TPU v7x, 32 devices: a whole 2x2x4 slice. The times are simulated.
32 devices in a mesh: gx: 4 (over z), gy: 2 (over y), gz: 4 (over x, core).
Axes of the slice: x: 2, y: 2, z: 4, core: 2. Of those that a mesh axis runs over, the one named last changes fastest.
Arguments:
- positions: float32 [3, 16, 8, 8, 128], P(None, 'gx', 'gy', 'gz'), may hold values from 0 to 1
- line_vectors: float32 [3, 16, 8, 8, 128], P(None, 'gx', 'gy', 'gz'), may hold values from -3 to 3
- burgers: float32 [3, 16, 8, 8, 128], P(None, 'gx', 'gy', 'gz'), may hold values from -6 to 6
- mobility: float32 [16, 8, 8, 128], P('gx', 'gy', 'gz'), may hold values from 0.25 to 4
- occupancy: int32 [16, 8, 8], P('gx', 'gy', 'gz'), may hold values from 1 to 128
Outputs:
- moved_positions: float32 [3, 16, 8, 8, 128], P(None, 'gx', 'gy', 'gz')
- end_forces: float32 [3, 16, 8, 8, 128], P(None, 'gx', 'gy', 'gz')
All inputs are finite; a program needn't handle non-finite values.
Results may differ from a plain program's by a relative error of at most 0.0001.
Values sent between devices are 32-bit elements; how exact they have to be, the bound alone decides.
A program may use at most 64 MiB of HBM per device.

v0:
```python
import jax
import jax.numpy as jnp
from jax import lax
from jax.sharding import PartitionSpec as P

CORE_SQUARED = 0.25
MU_SCALE = 0.05
CROSS_WEIGHT = 0.5
STEP_LIMIT = 0.1
CELL_BLOCK = 4
NEIGHBOUR_SHIFTS = [
    (first, second, third) for first in (-1, 0, 1) for second in (-1, 0, 1) for third in (-1, 0, 1)
]


def extended(block, sides, width):
    for axis, dim in sides:
        count = lax.axis_size(axis)
        forward = [(i, i + 1) for i in range(count - 1)]
        forward.append((count - 1, 0))
        backward = [(target, source) for source, target in forward]
        low = lax.ppermute(
            lax.slice_in_dim(block, block.shape[dim] - width, None, axis=dim), axis, forward
        )
        high = lax.ppermute(lax.slice_in_dim(block, 0, width, axis=dim), axis, backward)
        block = jnp.concatenate([low, block, high], axis=dim)
    return block


def inner_pairs(left, right):
    return sum((left[k][..., :, None] * right[k][..., None, :] for k in range(3)))


def tile_force(target, source):
    separate = [target[k][..., :, None] - source[k][..., None, :] for k in range(3)]
    radius_sq = (
        separate[0] * separate[0]
        + separate[1] * separate[1]
        + separate[2] * separate[2]
        + CORE_SQUARED
    )
    inverse = lax.rsqrt(radius_sq)
    couple = inner_pairs(target[6:9], source[6:9]) * inner_pairs(target[3:6], source[3:6])
    couple = couple - CROSS_WEIGHT * inner_pairs(target[6:9], source[3:6]) * inner_pairs(
        target[3:6], source[6:9]
    )
    weight = couple * source[9][..., None, :] * inverse * inverse * inverse
    return jnp.stack([jnp.sum(weight * separate[k], axis=-1) for k in range(3)]) * (
        MU_SCALE * target[9]
    )


def local_forces(fields, padded):
    width, count_x, count_y, count_z, slot_count = fields.shape
    pieces = []
    for offset in NEIGHBOUR_SHIFTS:
        source = padded[
            :,
            1 + offset[0] : 1 + offset[0] + count_x,
            1 + offset[1] : 1 + offset[1] + count_y,
            1 + offset[2] : 1 + offset[2] + count_z,
        ]
        shift_vec = jnp.array([float(offset[0]), float(offset[1]), float(offset[2])], jnp.float32)
        moved_src = source[0:3] + shift_vec[:, None, None, None, None]
        pieces.append(jnp.concatenate([moved_src, source[3:]], 0))
    sources = jnp.concatenate(pieces, 4)
    cell_count = count_x * count_y * count_z
    blocks = cell_count // CELL_BLOCK
    targets = jnp.moveaxis(fields.reshape(width, blocks, CELL_BLOCK, slot_count), 1, 0)
    sources = jnp.moveaxis(sources.reshape(width, blocks, CELL_BLOCK, sources.shape[4]), 1, 0)
    result = lax.map(lambda pair: tile_force(pair[0], pair[1]), (targets, sources))
    return jnp.moveaxis(result, 0, 1).reshape(3, count_x, count_y, count_z, slot_count)


def on_device(positions, line_vectors, burgers, mobility, occupancy):
    slots = lax.broadcasted_iota(jnp.int32, mobility.shape, 3)
    live = (slots < occupancy[..., None]).astype(jnp.float32)
    fixed_part = jnp.concatenate([line_vectors, burgers, live[None]], 0)
    fields = jnp.concatenate([positions, fixed_part], 0)
    padded = extended(fields, (("gx", 1), ("gy", 2), ("gz", 3)), 1)
    start_forces = local_forces(fields, padded)
    speed0 = mobility[None] * start_forces
    peak = lax.pmax(jnp.max(jnp.sum(speed0 * speed0, axis=0)), ("gx", "gy", "gz"))
    step = STEP_LIMIT * lax.rsqrt(peak + 1e-12)
    predicted = positions + step * speed0
    fields_next = jnp.concatenate([predicted, fixed_part], 0)
    moved_rim = extended(predicted, (("gx", 1), ("gy", 2), ("gz", 3)), 1)
    padded_next = jnp.concatenate([moved_rim, padded[3:]], 0)
    end_forces = local_forces(fields_next, padded_next)
    moved_positions = positions + 0.5 * step * (speed0 + mobility[None] * end_forces)
    return (moved_positions, end_forces)


def solution(mesh):
    return jax.shard_map(
        on_device,
        mesh=mesh,
        in_specs=(
            P(None, "gx", "gy", "gz", None),
            P(None, "gx", "gy", "gz", None),
            P(None, "gx", "gy", "gz", None),
            P("gx", "gy", "gz", None),
            P("gx", "gy", "gz"),
        ),
        out_specs=(P(None, "gx", "gy", "gz", None), P(None, "gx", "gy", "gz", None)),
        check_vma=False,
    )
```

profile of v0, /device:TPU:0, one launch (start us, length us, event | category | flops | bytes accessed | tf_op | source)
XLA Modules:
  0.0 349.4 jit_solution(12402889545487915617)
XLA Ops:
  0.7 0.8 copy.84
  1.7 0.9 pad_maximum_fusion.11
  2.6 3.1 collective-permute-start
  5.7 2.1 collective-permute-start.1
  8.0 0.9 fusion.19
  8.9 1.0 collective-permute-done
  10.2 0.9 pad_maximum_fusion.26
  11.0 1.6 collective-permute-start.2
  13.1 0.9 maximum_add_fusion.1
  14.1 1.2 collective-permute-done.2
  15.3 1.5 collective-permute-done.3
  16.8 1.0 pad_maximum_fusion.1
  18.2 1.7 collective-permute-start.5
  19.9 1.2 pad_maximum_fusion.2
  21.9 1.4 collective-permute-done.4
  24.1 1.2 pad_maximum_fusion
  25.4 0.9 fusion.28
  47.6 6.8 %reshape.339 = f32[10,8,4,3456]{3,2,1,0:T(4,128)} reshape(f32[10,4,4,2,3456]{4,3,2,1,0:T(2,128)} %maximum_dynamic-update-slice_fusion) | data formatting | bytes 8847360 | tf_op jit(solution)/shard_map/reshape | solution.py:70
  54.5 4.6 %copy.99 = f32[10,8,4,3456]{3,2,0,1:T(4,128)} copy(f32[10,8,4,3456]{3,2,1,0:T(4,128)} %reshape.339) | data formatting | bytes 8847360 | tf_op jit(solution)/shard_map/reshape | solution.py:70
  59.1 99.8 %while.20 = (s32[]{:T(128)}, f32[8,3,4,128]{3,2,1,0:T(4,128)S(1)}, f32[8,10,4,128]{3,2,0,1:T(4,128)S(1)}, f32[8,10,4,3456]{3,2,1,0:T(4,128)}, s32[]{:T(128)}, /*...) while((s32[]{:T(128)}, f32[8,3,4,128]{3,2,1,0:T(4,128)S(1)}, ...), condition=%wide.region_4.5_spmd, body=%wide.region_0.4_spmd.sunk | while | flops 76090888 | bytes 1780009 | solution.py:71
  59.1 1.1 dynamic-slice_bitcast_fusion.26
  60.3 11.3 %fusion.43 = (f32[4,128]{1,0:T(4,128)S(1)}, f32[4,128]{1,0:T(4,128)S(1)}, f32[4,128]{1,0:T(4,128)S(1)}) fusion(f32[4,3456]{1,0:T(4,128)S(1)} %get-tuple-element.334, f32[4,128]{1,0:T(4,128)S(1)} %get-tuple-element.335, f32[4,3456]{1,0:T(4,128)S(1)} %get-tuple-element.336, f32[4,128]{1,0:T(4,128)S(1)} %get-tuple-element.337, ...), kind=kLoop, calls=%fused_computation.11.clone.1 | loop fusion | flops 76085760 | bytes 577536 | tf_op jit(solution)/shard_map/while/body/eval_jaxpr/reduce_sum | solution.py:48
  71.6 1.1 dynamic-slice_bitcast_fusion.26
  72.8 11.3 %fusion.43 = (f32[4,128]{1,0:T(4,128)S(1)}, f32[4,128]{1,0:T(4,128)S(1)}, f32[4,128]{1,0:T(4,128)S(1)}) fusion(f32[4,3456]{1,0:T(4,128)S(1)} %get-tuple-element.334, f32[4,128]{1,0:T(4,128)S(1)} %get-tuple-element.335, f32[4,3456]{1,0:T(4,128)S(1)} %get-tuple-element.336, f32[4,128]{1,0:T(4,128)S(1)} %get-tuple-element.337, ...), kind=kLoop, calls=%fused_computation.11.clone.1 | loop fusion | flops 76085760 | bytes 577536 | tf_op jit(solution)/shard_map/while/body/eval_jaxpr/reduce_sum | solution.py:48
  84.1 1.1 dynamic-slice_bitcast_fusion.26
  85.2 11.3 %fusion.43 = (f32[4,128]{1,0:T(4,128)S(1)}, f32[4,128]{1,0:T(4,128)S(1)}, f32[4,128]{1,0:T(4,128)S(1)}) fusion(f32[4,3456]{1,0:T(4,128)S(1)} %get-tuple-element.334, f32[4,128]{1,0:T(4,128)S(1)} %get-tuple-element.335, f32[4,3456]{1,0:T(4,128)S(1)} %get-tuple-element.336, f32[4,128]{1,0:T(4,128)S(1)} %get-tuple-element.337, ...), kind=kLoop, calls=%fused_computation.11.clone.1 | loop fusion | flops 76085760 | bytes 577536 | tf_op jit(solution)/shard_map/while/body/eval_jaxpr/reduce_sum | solution.py:48
  96.6 1.1 dynamic-slice_bitcast_fusion.26
  97.7 11.3 %fusion.43 = (f32[4,128]{1,0:T(4,128)S(1)}, f32[4,128]{1,0:T(4,128)S(1)}, f32[4,128]{1,0:T(4,128)S(1)}) fusion(f32[4,3456]{1,0:T(4,128)S(1)} %get-tuple-element.334, f32[4,128]{1,0:T(4,128)S(1)} %get-tuple-element.335, f32[4,3456]{1,0:T(4,128)S(1)} %get-tuple-element.336, f32[4,128]{1,0:T(4,128)S(1)} %get-tuple-element.337, ...), kind=kLoop, calls=%fused_computation.11.clone.1 | loop fusion | flops 76085760 | bytes 577536 | tf_op jit(solution)/shard_map/while/body/eval_jaxpr/reduce_sum | solution.py:48
  109.0 1.1 dynamic-slice_bitcast_fusion.26
  110.2 11.3 %fusion.43 = (f32[4,128]{1,0:T(4,128)S(1)}, f32[4,128]{1,0:T(4,128)S(1)}, f32[4,128]{1,0:T(4,128)S(1)}) fusion(f32[4,3456]{1,0:T(4,128)S(1)} %get-tuple-element.334, f32[4,128]{1,0:T(4,128)S(1)} %get-tuple-element.335, f32[4,3456]{1,0:T(4,128)S(1)} %get-tuple-element.336, f32[4,128]{1,0:T(4,128)S(1)} %get-tuple-element.337, ...), kind=kLoop, calls=%fused_computation.11.clone.1 | loop fusion | flops 76085760 | bytes 577536 | tf_op jit(solution)/shard_map/while/body/eval_jaxpr/reduce_sum | solution.py:48
  121.5 1.1 dynamic-slice_bitcast_fusion.26
  122.7 11.3 %fusion.43 = (f32[4,128]{1,0:T(4,128)S(1)}, f32[4,128]{1,0:T(4,128)S(1)}, f32[4,128]{1,0:T(4,128)S(1)}) fusion(f32[4,3456]{1,0:T(4,128)S(1)} %get-tuple-element.334, f32[4,128]{1,0:T(4,128)S(1)} %get-tuple-element.335, f32[4,3456]{1,0:T(4,128)S(1)} %get-tuple-element.336, f32[4,128]{1,0:T(4,128)S(1)} %get-tuple-element.337, ...), kind=kLoop, calls=%fused_computation.11.clone.1 | loop fusion | flops 76085760 | bytes 577536 | tf_op jit(solution)/shard_map/while/body/eval_jaxpr/reduce_sum | solution.py:48
  134.0 1.1 dynamic-slice_bitcast_fusion.26
  135.1 11.3 %fusion.43 = (f32[4,128]{1,0:T(4,128)S(1)}, f32[4,128]{1,0:T(4,128)S(1)}, f32[4,128]{1,0:T(4,128)S(1)}) fusion(f32[4,3456]{1,0:T(4,128)S(1)} %get-tuple-element.334, f32[4,128]{1,0:T(4,128)S(1)} %get-tuple-element.335, f32[4,3456]{1,0:T(4,128)S(1)} %get-tuple-element.336, f32[4,128]{1,0:T(4,128)S(1)} %get-tuple-element.337, ...), kind=kLoop, calls=%fused_computation.11.clone.1 | loop fusion | flops 76085760 | bytes 577536 | tf_op jit(solution)/shard_map/while/body/eval_jaxpr/reduce_sum | solution.py:48
  146.4 1.1 dynamic-slice_bitcast_fusion.26
  147.6 11.3 %fusion.43 = (f32[4,128]{1,0:T(4,128)S(1)}, f32[4,128]{1,0:T(4,128)S(1)}, f32[4,128]{1,0:T(4,128)S(1)}) fusion(f32[4,3456]{1,0:T(4,128)S(1)} %get-tuple-element.334, f32[4,128]{1,0:T(4,128)S(1)} %get-tuple-element.335, f32[4,3456]{1,0:T(4,128)S(1)} %get-tuple-element.336, f32[4,128]{1,0:T(4,128)S(1)} %get-tuple-element.337, ...), kind=kLoop, calls=%fused_computation.11.clone.1 | loop fusion | flops 76085760 | bytes 577536 | tf_op jit(solution)/shard_map/while/body/eval_jaxpr/reduce_sum | solution.py:48
  159.6 39.7 %pmax.7 = f32[]{:T(128)} all-reduce(f32[]{:T(128)} %reduce_max.9), channel_id=1, replica_groups=mesh['gx'=4,'gy'=2,'gz'=4] {'gx','gy','gz'}, use_global_device_ids=true, to_apply=%region_7.8 | all-reduce | flops 1 | bytes 8 | tf_op jit(solution)/shard_map/pmax | solution.py:83
  200.0 2.1 collective-permute-start.6
  202.1 1.8 collective-permute-start.7
  203.9 1.6 collective-permute-done.6
  205.8 2.5 collective-permute-start.8
  208.5 1.6 collective-permute-done.8
  210.1 2.0 collective-permute-done.9
  212.5 1.7 collective-permute-start.11
  214.3 1.7 collective-permute-done.10
  237.5 6.8 %reshape.341 = f32[10,8,4,3456]{3,2,1,0:T(4,128)} reshape(f32[10,4,4,2,3456]{4,3,2,1,0:T(2,128)} %maximum_dynamic-update-slice_fusion.26) | data formatting | bytes 8847360 | tf_op jit(solution)/shard_map/reshape | solution.py:70
  244.3 4.6 %copy.98 = f32[10,8,4,3456]{3,2,0,1:T(4,128)} copy(f32[10,8,4,3456]{3,2,1,0:T(4,128)} %reshape.341) | data formatting | bytes 8847360 | tf_op jit(solution)/shard_map/reshape | solution.py:70
  248.9 99.8 %while.21 = (s32[]{:T(128)}, f32[8,3,4,128]{3,2,1,0:T(4,128)S(1)}, f32[8,10,4,128]{3,2,0,1:T(4,128)S(1)}, f32[8,10,4,3456]{3,2,1,0:T(4,128)}, s32[]{:T(128)}, /*...) while((s32[]{:T(128)}, f32[8,3,4,128]{3,2,1,0:T(4,128)S(1)}, ...), condition=%wide.region_12.13_spmd, body=%wide.region_8.12_spmd.sunk | while | flops 76090888 | bytes 1780009 | solution.py:71
  248.9 1.1 dynamic-slice_bitcast_fusion.28
  250.1 11.3 %fusion.46 = (f32[4,128]{1,0:T(4,128)S(1)}, f32[4,128]{1,0:T(4,128)S(1)}, f32[4,128]{1,0:T(4,128)S(1)}) fusion(f32[4,3456]{1,0:T(4,128)S(1)} %get-tuple-element.361, f32[4,128]{1,0:T(4,128)S(1)} %get-tuple-element.362, f32[4,3456]{1,0:T(4,128)S(1)} %get-tuple-element.363, f32[4,128]{1,0:T(4,128)S(1)} %get-tuple-element.364, ...), kind=kLoop, calls=%fused_computation.49.clone.1 | loop fusion | flops 76085760 | bytes 577536 | tf_op jit(solution)/shard_map/while/body/eval_jaxpr/reduce_sum | solution.py:48
  261.4 1.1 dynamic-slice_bitcast_fusion.28
  262.6 11.3 %fusion.46 = (f32[4,128]{1,0:T(4,128)S(1)}, f32[4,128]{1,0:T(4,128)S(1)}, f32[4,128]{1,0:T(4,128)S(1)}) fusion(f32[4,3456]{1,0:T(4,128)S(1)} %get-tuple-element.361, f32[4,128]{1,0:T(4,128)S(1)} %get-tuple-element.362, f32[4,3456]{1,0:T(4,128)S(1)} %get-tuple-element.363, f32[4,128]{1,0:T(4,128)S(1)} %get-tuple-element.364, ...), kind=kLoop, calls=%fused_computation.49.clone.1 | loop fusion | flops 76085760 | bytes 577536 | tf_op jit(solution)/shard_map/while/body/eval_jaxpr/reduce_sum | solution.py:48
  273.9 1.1 dynamic-slice_bitcast_fusion.28
  275.1 11.3 %fusion.46 = (f32[4,128]{1,0:T(4,128)S(1)}, f32[4,128]{1,0:T(4,128)S(1)}, f32[4,128]{1,0:T(4,128)S(1)}) fusion(f32[4,3456]{1,0:T(4,128)S(1)} %get-tuple-element.361, f32[4,128]{1,0:T(4,128)S(1)} %get-tuple-element.362, f32[4,3456]{1,0:T(4,128)S(1)} %get-tuple-element.363, f32[4,128]{1,0:T(4,128)S(1)} %get-tuple-element.364, ...), kind=kLoop, calls=%fused_computation.49.clone.1 | loop fusion | flops 76085760 | bytes 577536 | tf_op jit(solution)/shard_map/while/body/eval_jaxpr/reduce_sum | solution.py:48
  286.4 1.1 dynamic-slice_bitcast_fusion.28
  287.5 11.3 %fusion.46 = (f32[4,128]{1,0:T(4,128)S(1)}, f32[4,128]{1,0:T(4,128)S(1)}, f32[4,128]{1,0:T(4,128)S(1)}) fusion(f32[4,3456]{1,0:T(4,128)S(1)} %get-tuple-element.361, f32[4,128]{1,0:T(4,128)S(1)} %get-tuple-element.362, f32[4,3456]{1,0:T(4,128)S(1)} %get-tuple-element.363, f32[4,128]{1,0:T(4,128)S(1)} %get-tuple-element.364, ...), kind=kLoop, calls=%fused_computation.49.clone.1 | loop fusion | flops 76085760 | bytes 577536 | tf_op jit(solution)/shard_map/while/body/eval_jaxpr/reduce_sum | solution.py:48
  298.9 1.1 dynamic-slice_bitcast_fusion.28
  300.0 11.3 %fusion.46 = (f32[4,128]{1,0:T(4,128)S(1)}, f32[4,128]{1,0:T(4,128)S(1)}, f32[4,128]{1,0:T(4,128)S(1)}) fusion(f32[4,3456]{1,0:T(4,128)S(1)} %get-tuple-element.361, f32[4,128]{1,0:T(4,128)S(1)} %get-tuple-element.362, f32[4,3456]{1,0:T(4,128)S(1)} %get-tuple-element.363, f32[4,128]{1,0:T(4,128)S(1)} %get-tuple-element.364, ...), kind=kLoop, calls=%fused_computation.49.clone.1 | loop fusion | flops 76085760 | bytes 577536 | tf_op jit(solution)/shard_map/while/body/eval_jaxpr/reduce_sum | solution.py:48
  311.3 1.1 dynamic-slice_bitcast_fusion.28
  312.5 11.3 %fusion.46 = (f32[4,128]{1,0:T(4,128)S(1)}, f32[4,128]{1,0:T(4,128)S(1)}, f32[4,128]{1,0:T(4,128)S(1)}) fusion(f32[4,3456]{1,0:T(4,128)S(1)} %get-tuple-element.361, f32[4,128]{1,0:T(4,128)S(1)} %get-tuple-element.362, f32[4,3456]{1,0:T(4,128)S(1)} %get-tuple-element.363, f32[4,128]{1,0:T(4,128)S(1)} %get-tuple-element.364, ...), kind=kLoop, calls=%fused_computation.49.clone.1 | loop fusion | flops 76085760 | bytes 577536 | tf_op jit(solution)/shard_map/while/body/eval_jaxpr/reduce_sum | solution.py:48
  323.8 1.1 dynamic-slice_bitcast_fusion.28
  325.0 11.3 %fusion.46 = (f32[4,128]{1,0:T(4,128)S(1)}, f32[4,128]{1,0:T(4,128)S(1)}, f32[4,128]{1,0:T(4,128)S(1)}) fusion(f32[4,3456]{1,0:T(4,128)S(1)} %get-tuple-element.361, f32[4,128]{1,0:T(4,128)S(1)} %get-tuple-element.362, f32[4,3456]{1,0:T(4,128)S(1)} %get-tuple-element.363, f32[4,128]{1,0:T(4,128)S(1)} %get-tuple-element.364, ...), kind=kLoop, calls=%fused_computation.49.clone.1 | loop fusion | flops 76085760 | bytes 577536 | tf_op jit(solution)/shard_map/while/body/eval_jaxpr/reduce_sum | solution.py:48
  336.3 1.1 dynamic-slice_bitcast_fusion.28
  337.5 11.3 %fusion.46 = (f32[4,128]{1,0:T(4,128)S(1)}, f32[4,128]{1,0:T(4,128)S(1)}, f32[4,128]{1,0:T(4,128)S(1)}) fusion(f32[4,3456]{1,0:T(4,128)S(1)} %get-tuple-element.361, f32[4,128]{1,0:T(4,128)S(1)} %get-tuple-element.362, f32[4,3456]{1,0:T(4,128)S(1)} %get-tuple-element.363, f32[4,128]{1,0:T(4,128)S(1)} %get-tuple-element.364, ...), kind=kLoop, calls=%fused_computation.49.clone.1 | loop fusion | flops 76085760 | bytes 577536 | tf_op jit(solution)/shard_map/while/body/eval_jaxpr/reduce_sum | solution.py:48
  (199 shorter events, 48.4 us)
Async XLA Ops:
  0.6 20.8 %copy-start.24 = (f32[3]{0:T(128)S(1)}, f32[3]{0:T(128)}, u32[]{:S(2)}) copy-start(f32[3]{0:T(128)} %constant.104.clone) | copy-start | bytes 40
  0.6 20.8 %copy-start.21 = (f32[3]{0:T(128)S(1)}, f32[3]{0:T(128)}, u32[]{:S(2)}) copy-start(f32[3]{0:T(128)} %constant.110.clone) | copy-start | bytes 40
  0.7 20.9 %copy-start.25 = (f32[3]{0:T(128)S(1)}, f32[3]{0:T(128)}, u32[]{:S(2)}) copy-start(f32[3]{0:T(128)} %constant.113.clone) | copy-start | bytes 40
  0.7 20.9 %copy-start.26 = (f32[3]{0:T(128)S(1)}, f32[3]{0:T(128)}, u32[]{:S(2)}) copy-start(f32[3]{0:T(128)} %constant.122.clone) | copy-start | bytes 40
  0.7 21.1 %copy-start.22 = (f32[3]{0:T(128)S(1)}, f32[3]{0:T(128)}, u32[]{:S(2)}) copy-start(f32[3]{0:T(128)} %constant.119.clone) | copy-start | bytes 40
  0.7 21.1 %copy-start.23 = (f32[3]{0:T(128)S(1)}, f32[3]{0:T(128)}, u32[]{:S(2)}) copy-start(f32[3]{0:T(128)} %constant.128.clone) | copy-start | bytes 40
  0.7 20.7 %copy-start.2 = (f32[3,4,4,2,128]{4,3,2,1,0:T(2,128)S(1)}, f32[3,4,4,2,128]{4,3,2,1,0:T(2,128)}, u32[]{:S(2)}) copy-start(f32[3,4,4,2,128]{4,3,2,1,0:T(2,128)} %param.63) | copy-start | bytes 147460
  0.7 20.7 %copy-start.1 = (f32[3,4,4,2,128]{4,3,2,1,0:T(2,128)S(1)}, f32[3,4,4,2,128]{4,3,2,1,0:T(2,128)}, u32[]{:S(2)}) copy-start(f32[3,4,4,2,128]{4,3,2,1,0:T(2,128)} %param.64) | copy-start | bytes 147460
  0.7 20.7 %copy-start = (f32[3,4,4,2,128]{4,3,2,1,0:T(2,128)S(1)}, f32[3,4,4,2,128]{4,3,2,1,0:T(2,128)}, u32[]{:S(2)}) copy-start(f32[3,4,4,2,128]{4,3,2,1,0:T(2,128)} %param.65) | copy-start | bytes 147460
  2.6 7.2 %collective-permute-start = (f32[10,1,4,2,128]{4,3,2,1,0:T(2,128)S(1)}, f32[10,1,4,2,128]{4,3,2,1,0:T(2,128)S(1)}, u32[]{:S(2)}, u32[]{:S(2)}) collective-permute-start(f32[10,1,4,2,128]{4,3,2,1,0:T(2,128)S(1)} %get-tuple-element.210), channel_id=1, source_target_pairs={{0,8},{8,16},{16,24},{24,0},{1,9},{9,17},{17,25},{25,1},{2,10},{10... | collective-permute-start | bytes 122888 | tf_op jit(solution)/shard_map/ppermute | solution.py:22
  5.7 4.4 %collective-permute-start.1 = (f32[10,1,4,2,128]{4,3,2,1,0:T(2,128)S(1)}, f32[10,1,4,2,128]{4,3,2,1,0:T(2,128)S(1)}, u32[]{:S(2)}, u32[]{:S(2)}) collective-permute-start(f32[10,1,4,2,128]{4,3,2,1,0:T(2,128)S(1)} %get-tuple-element.211), channel_id=1, source_target_pairs={{8,0},{16,8},{24,16},{0,24},{9,1},{17,9},{25,17},{1,25},{10,2},{18... | collective-permute-start | bytes 122888 | tf_op jit(solution)/shard_map/ppermute | solution.py:25
  11.0 4.3 %collective-permute-start.2 = (f32[10,6,1,2,128]{4,3,2,1,0:T(2,128)S(1)}, f32[10,6,1,2,128]{4,3,2,1,0:T(2,128)S(1)}, u32[]{:S(2)}, u32[]{:S(2)}) collective-permute-start(f32[10,6,1,2,128]{4,3,2,1,0:T(2,128)S(1)} %get-tuple-element.188), channel_id=1, source_target_pairs={{0,4},{4,0},{1,5},{5,1},{2,6},{6,2},{3,7},{7,3},{8,12},{12,8},{9,1... | collective-permute-start | bytes 184328 | tf_op jit(solution)/shard_map/ppermute | solution.py:22
  12.6 4.2 %collective-permute-start.3 = (f32[10,6,1,2,128]{4,3,2,1,0:T(2,128)S(1)}, f32[10,6,1,2,128]{4,3,2,1,0:T(2,128)S(1)}, u32[]{:S(2)}, u32[]{:S(2)}) collective-permute-start(f32[10,6,1,2,128]{4,3,2,1,0:T(2,128)S(1)} %get-tuple-element.189), channel_id=1, source_target_pairs={{4,0},{0,4},{5,1},{1,5},{6,2},{2,6},{7,3},{3,7},{12,8},{8,12},{13,... | collective-permute-start | bytes 184328 | tf_op jit(solution)/shard_map/ppermute | solution.py:25
  18.1 5.2 %collective-permute-start.4 = (f32[10,6,6,1,128]{4,3,2,1,0:T(1,128)S(1)}, f32[10,6,6,1,128]{4,3,2,1,0:T(1,128)S(1)}, u32[]{:S(2)}, u32[]{:S(2)}) collective-permute-start(f32[10,6,6,1,128]{4,3,2,1,0:T(1,128)S(1)} %get-tuple-element.173), channel_id=1, source_target_pairs={{0,1},{1,2},{2,3},{3,0},{4,5},{5,6},{6,7},{7,4},{8,9},{9,10},{10,1... | collective-permute-start | bytes 552968 | tf_op jit(solution)/shard_map/ppermute | solution.py:22
  18.2 5.9 %collective-permute-start.5 = (f32[10,6,6,1,128]{4,3,2,1,0:T(1,128)S(1)}, f32[10,6,6,1,128]{4,3,2,1,0:T(1,128)S(1)}, u32[]{:S(2)}, u32[]{:S(2)}) collective-permute-start(f32[10,6,6,1,128]{4,3,2,1,0:T(1,128)S(1)} %get-tuple-element.172), channel_id=1, source_target_pairs={{1,0},{2,1},{3,2},{0,3},{5,4},{6,5},{7,6},{4,7},{9,8},{10,9},{11,1... | collective-permute-start | bytes 552968 | tf_op jit(solution)/shard_map/ppermute | solution.py:25
  21.1 5.2 %copy-start.13 = (f32[3]{0:T(128)S(1)}, f32[3]{0:T(128)}, u32[]{:S(2)}) copy-start(f32[3]{0:T(128)} %constant.106.clone) | copy-start | bytes 40
  21.1 5.2 %copy-start.14 = (f32[3]{0:T(128)S(1)}, f32[3]{0:T(128)}, u32[]{:S(2)}) copy-start(f32[3]{0:T(128)} %constant.109.clone) | copy-start | bytes 40
  21.1 5.2 %copy-start.15 = (f32[3]{0:T(128)S(1)}, f32[3]{0:T(128)}, u32[]{:S(2)}) copy-start(f32[3]{0:T(128)} %constant.112.clone) | copy-start | bytes 40
  21.2 5.2 %copy-start.16 = (f32[3]{0:T(128)S(1)}, f32[3]{0:T(128)}, u32[]{:S(2)}) copy-start(f32[3]{0:T(128)} %constant.115.clone) | copy-start | bytes 40
  21.2 5.2 %copy-start.17 = (f32[3]{0:T(128)S(1)}, f32[3]{0:T(128)}, u32[]{:S(2)}) copy-start(f32[3]{0:T(128)} %constant.118.clone) | copy-start | bytes 40
  21.2 5.2 %copy-start.18 = (f32[3]{0:T(128)S(1)}, f32[3]{0:T(128)}, u32[]{:S(2)}) copy-start(f32[3]{0:T(128)} %constant.121.clone) | copy-start | bytes 40
  21.2 5.2 %copy-start.19 = (f32[3]{0:T(128)S(1)}, f32[3]{0:T(128)}, u32[]{:S(2)}) copy-start(f32[3]{0:T(128)} %constant.124.clone) | copy-start | bytes 40
  21.2 5.2 %copy-start.20 = (f32[3]{0:T(128)S(1)}, f32[3]{0:T(128)}, u32[]{:S(2)}) copy-start(f32[3]{0:T(128)} %constant.127.clone) | copy-start | bytes 40
  21.6 6.5 %copy-start.5 = (f32[3]{0:T(128)S(1)}, f32[3]{0:T(128)}, u32[]{:S(2)}) copy-start(f32[3]{0:T(128)} %constant.105.clone) | copy-start | bytes 40
  21.6 6.5 %copy-start.6 = (f32[3]{0:T(128)S(1)}, f32[3]{0:T(128)}, u32[]{:S(2)}) copy-start(f32[3]{0:T(128)} %constant.108.clone) | copy-start | bytes 40
  21.6 6.5 %copy-start.7 = (f32[3]{0:T(128)S(1)}, f32[3]{0:T(128)}, u32[]{:S(2)}) copy-start(f32[3]{0:T(128)} %constant.111.clone) | copy-start | bytes 40
  21.6 6.4 %copy-start.8 = (f32[3]{0:T(128)S(1)}, f32[3]{0:T(128)}, u32[]{:S(2)}) copy-start(f32[3]{0:T(128)} %constant.114.clone) | copy-start | bytes 40
  21.6 6.4 %copy-start.9 = (f32[3]{0:T(128)S(1)}, f32[3]{0:T(128)}, u32[]{:S(2)}) copy-start(f32[3]{0:T(128)} %constant.117.clone) | copy-start | bytes 40
  21.6 6.4 %copy-start.10 = (f32[3]{0:T(128)S(1)}, f32[3]{0:T(128)}, u32[]{:S(2)}) copy-start(f32[3]{0:T(128)} %constant.120.clone) | copy-start | bytes 40
  21.7 6.4 %copy-start.11 = (f32[3]{0:T(128)S(1)}, f32[3]{0:T(128)}, u32[]{:S(2)}) copy-start(f32[3]{0:T(128)} %constant.123.clone) | copy-start | bytes 40
  21.7 6.4 %copy-start.12 = (f32[3]{0:T(128)S(1)}, f32[3]{0:T(128)}, u32[]{:S(2)}) copy-start(f32[3]{0:T(128)} %constant.126.clone) | copy-start | bytes 40
  59.1 99.8 %copy-start.4 = (f32[4,4,2,128]{3,2,1,0:T(2,128)S(1)}, f32[4,4,2,128]{3,2,1,0:T(2,128)}, u32[]{:S(2)}) copy-start(f32[4,4,2,128]{3,2,1,0:T(2,128)} %param.66) | copy-start | bytes 49156
  59.1 149.3 %copy-start.27 = (f32[3]{0:T(128)S(1)}, f32[3]{0:T(128)}, u32[]{:S(2)}) copy-start(f32[3]{0:T(128)} %constant.107.clone) | copy-start | bytes 40
  59.1 149.3 %copy-start.28 = (f32[3]{0:T(128)S(1)}, f32[3]{0:T(128)}, u32[]{:S(2)}) copy-start(f32[3]{0:T(128)} %constant.125.clone) | copy-start | bytes 40
  200.0 5.5 %collective-permute-start.6 = (f32[3,1,4,2,128]{4,3,2,1,0:T(2,128)S(1)}, f32[3,1,4,2,128]{4,3,2,1,0:T(2,128)S(1)}, u32[]{:S(2)}, u32[]{:S(2)}) collective-permute-start(f32[3,1,4,2,128]{4,3,2,1,0:T(2,128)S(1)} %get-tuple-element.228), channel_id=1, source_target_pairs={{0,8},{8,16},{16,24},{24,0},{1,9},{9,17},{17,25},{25,1},{2,10},{10... | collective-permute-start | bytes 36872 | tf_op jit(solution)/shard_map/ppermute | solution.py:22
  202.1 3.7 %collective-permute-start.7 = (f32[3,1,4,2,128]{4,3,2,1,0:T(2,128)S(1)}, f32[3,1,4,2,128]{4,3,2,1,0:T(2,128)S(1)}, u32[]{:S(2)}, u32[]{:S(2)}) collective-permute-start(f32[3,1,4,2,128]{4,3,2,1,0:T(2,128)S(1)} %get-tuple-element.229), channel_id=1, source_target_pairs={{8,0},{16,8},{24,16},{0,24},{9,1},{17,9},{25,17},{1,25},{10,2},{18... | collective-permute-start | bytes 36872 | tf_op jit(solution)/shard_map/ppermute | solution.py:25
  205.8 4.3 %collective-permute-start.8 = (f32[3,6,1,2,128]{4,3,2,1,0:T(2,128)S(1)}, f32[3,6,1,2,128]{4,3,2,1,0:T(2,128)S(1)}, u32[]{:S(2)}, u32[]{:S(2)}) collective-permute-start(f32[3,6,1,2,128]{4,3,2,1,0:T(2,128)S(1)} %get-tuple-element.224), channel_id=1, source_target_pairs={{0,4},{4,0},{1,5},{5,1},{2,6},{6,2},{3,7},{7,3},{8,12},{12,8},{9,1... | collective-permute-start | bytes 55304 | tf_op jit(solution)/shard_map/ppermute | solution.py:22
  208.3 3.8 %collective-permute-start.9 = (f32[3,6,1,2,128]{4,3,2,1,0:T(2,128)S(1)}, f32[3,6,1,2,128]{4,3,2,1,0:T(2,128)S(1)}, u32[]{:S(2)}, u32[]{:S(2)}) collective-permute-start(f32[3,6,1,2,128]{4,3,2,1,0:T(2,128)S(1)} %get-tuple-element.225), channel_id=1, source_target_pairs={{4,0},{0,4},{5,1},{1,5},{6,2},{2,6},{7,3},{3,7},{12,8},{8,12},{13,... | collective-permute-start | bytes 55304 | tf_op jit(solution)/shard_map/ppermute | solution.py:25
  212.4 3.6 %collective-permute-start.10 = (f32[3,6,6,1,128]{4,3,2,1,0:T(1,128)S(1)}, f32[3,6,6,1,128]{4,3,2,1,0:T(1,128)S(1)}, u32[]{:S(2)}, u32[]{:S(2)}) collective-permute-start(f32[3,6,6,1,128]{4,3,2,1,0:T(1,128)S(1)} %get-tuple-element.215), channel_id=1, source_target_pairs={{0,1},{1,2},{2,3},{3,0},{4,5},{5,6},{6,7},{7,4},{8,9},{9,10},{10,1... | collective-permute-start | bytes 165896 | tf_op jit(solution)/shard_map/ppermute | solution.py:22
  212.5 3.6 %collective-permute-start.11 = (f32[3,6,6,1,128]{4,3,2,1,0:T(1,128)S(1)}, f32[3,6,6,1,128]{4,3,2,1,0:T(1,128)S(1)}, u32[]{:S(2)}, u32[]{:S(2)}) collective-permute-start(f32[3,6,6,1,128]{4,3,2,1,0:T(1,128)S(1)} %get-tuple-element.214), channel_id=1, source_target_pairs={{1,0},{2,1},{3,2},{0,3},{5,4},{6,5},{7,6},{4,7},{9,8},{10,9},{11,1... | collective-permute-start | bytes 165896 | tf_op jit(solution)/shard_map/ppermute | solution.py:25
  348.8 0.7 copy-start.3
where the time goes:
time: 352 us; the launch traced here: 349 us
  other arithmetic  233 us (66%)
  local copies, waits for them, and re-layouts  43.6 us (12%)
  blocking collectives  39.7 us (11%)
  starting transfers between devices  17.4 us (5%)
  waiting for transfers between devices  13.4 us (4%)
    reduce_sum x16, other arithmetic, tile_force(): jnp.sum(weight * separate[k], axis=-1)  180 us
    unnamed x52, other arithmetic  40.2 us
    pmax x1, blocking collectives, on_device(): lax.pmax(jnp.max(jnp.sum(speed0 * speed0, axis=0)), ('gx', 'gy', 'gz'))  39.7 us
    reshape x4, local copies, waits for them, and re-layouts, local_forces(): sources.reshape(width, blocks, CELL_BLOCK, sources.shape[4])  22.8 us
    mul x16, local copies, waits for them, and re-layouts, inner_pairs(): left[k][..., :, None] * right[k][..., None, :]  17.9 us
    ppermute x6, starting transfers between devices, extended(): lax.ppermute(lax.slice_in_dim(block, block.shape[dim] - width, None, axis...  9.41 us
    ppermute x6, waiting for transfers between devices, extended(): lax.ppermute(lax.slice_in_dim(block, block.shape[dim] - width, None, axis...  8.55 us
    ppermute x6, starting transfers between devices, extended(): lax.ppermute(lax.slice_in_dim(block, 0, width, axis=dim), axis, backward)  7.94 us
  transfers between devices with their start and end apart: 12, of which 11 were waited for; matrix products, arithmetic and copies ran while one was open for 1% of the time, Pallas kernels for 0%

commit v1 on v0

v1 whole, which is shorter than its diff:
```python
import functools

import jax
import jax.numpy as jnp
from jax import lax
from jax.experimental import pallas as pl
from jax.experimental.pallas import tpu as pltpu
from jax.sharding import PartitionSpec as P

CORE_SQUARED = 0.25
MU_SCALE = 0.05
CROSS_WEIGHT = 0.5
STEP_LIMIT = 0.1
AXES = ("gx", "gy", "gz")
K_ROWS = 72


def extended(block):
    for dim, axis in enumerate(AXES):
        count = lax.axis_size(axis)
        forward = [(i, (i + 1) % count) for i in range(count)]
        backward = [(target, source) for source, target in forward]
        low = lax.ppermute(
            lax.slice_in_dim(block, block.shape[dim] - 1, None, axis=dim), axis, forward
        )
        high = lax.ppermute(lax.slice_in_dim(block, 0, 1, axis=dim), axis, backward)
        block = jnp.concatenate([low, block, high], axis=dim)
    return block


def split(value, parts):
    terms = []
    for _ in range(parts):
        term = value.astype(jnp.bfloat16).astype(jnp.float32)
        terms.append(term)
        value = value - term
    return terms


def offsets(row, index, local):
    corner = [i.astype(jnp.float32) - (1.0 + n / 2) for i, n in zip(index, local)]
    return jnp.where(row == 0, corner[0], jnp.where(row == 1, corner[1], corner[2]))


def source_rows(fix, place, row):
    live = fix[3:4]
    turned = pltpu.roll(fix, 4, 0)
    keep = jnp.where(row < 3, live, 0.0)
    lines, burgers = fix * keep, turned * keep
    high, low = [], []
    for a in range(3):
        form = fix[4 + a : 5 + a] * lines - CROSS_WEIGHT * fix[a : a + 1] * burgers
        first, second = split(form, 2)
        high.append(first)
        low.append(second)
    square = jnp.sum(place * place, axis=0, keepdims=True) + CORE_SQUARED
    vec = jnp.where(row < 3, place, jnp.where(row == 3, square, jnp.where(row == 4, 1.0, 0.0)))
    h, m, l = split(vec, 3)
    zero = jnp.zeros_like(h)
    return jnp.concatenate(high + low + high + [h, m, h, m, l, h, zero], axis=0)


def target_rows(fix, place, row):
    high, low = [], []
    for a in range(3):
        first, second = split(fix[4 + a : 5 + a] * fix, 2)
        high.append(first)
        low.append(second)
    square = jnp.sum(place * place, axis=0, keepdims=True)
    vec = jnp.where(
        row < 3, -2.0 * place, jnp.where(row == 3, 1.0, jnp.where(row == 4, square, 0.0))
    )
    h, m, l = split(vec, 3)
    zero = jnp.zeros_like(h)
    return jnp.concatenate(high + high + low + [h, h, m, m, h, l, zero], axis=0)


def sweep(local, slots, occ_ref, fix_ref, pos_ref, base_ref, place_ref, lhs_ref, acc_ref, emit):
    ext = tuple(n + 2 for n in local)
    row = lax.broadcasted_iota(jnp.int32, (8, slots), 0)

    def prepare(c, carry):
        z = lax.rem(c, ext[2])
        y = lax.rem(c // ext[2], ext[1])
        x = c // (ext[2] * ext[1])
        place = jnp.where(row < 3, pos_ref[x, y, z] + offsets(row, (x, y, z), local), 0.0)
        place_ref[x, y, z] = place
        base_ref[x, y, z] = source_rows(fix_ref[x, y, z], place, row).astype(jnp.bfloat16)
        return carry

    lax.fori_loop(0, ext[0] * ext[1] * ext[2], prepare, 0)

    def one_cell(c, carry):
        z = lax.rem(c, local[2])
        y = lax.rem(c // local[2], local[1])
        x = c // (local[2] * local[1])
        fix = fix_ref[x + 1, y + 1, z + 1]
        place = place_ref[x + 1, y + 1, z + 1]
        turned = target_rows(fix, place, row).T
        lane = lax.broadcasted_iota(jnp.int32, turned.shape, 1)
        lhs_ref[0] = jnp.where(lane < K_ROWS, turned, 0.0).astype(jnp.bfloat16)
        lhs_ref[1] = jnp.where(lane < K_ROWS, 0.0, turned).astype(jnp.bfloat16)
        acc_ref[...] = jnp.zeros_like(acc_ref)
        groups = (occ_ref[x, y, z] + 31) // 32

        for group in range(1, slots // 32 + 1):

            @pl.when(groups == group)
            def _():
                rows = 32 * group
                lhs = jnp.concatenate([lhs_ref[0, :rows], lhs_ref[1, :rows]], axis=0)

                def column(i, carry):
                    sx = x + i // 3
                    sy = y + lax.rem(i, 3)
                    rhs = jnp.concatenate([base_ref[sx, sy, z + d] for d in range(3)], axis=1)
                    both = jnp.dot(lhs, rhs, preferred_element_type=jnp.float32)
                    inverse = lax.rsqrt(both[rows:])
                    weight = both[:rows] * (inverse * inverse * inverse)
                    sums = [0.0] * 4
                    for d in range(3):
                        part = weight[:, d * slots : (d + 1) * slots]
                        sums[3] = sums[3] + part
                        for k in range(3):
                            coord = place_ref[sx, sy, z + d, k : k + 1]
                            sums[k] = sums[k] + part * coord
                    for k in range(4):
                        acc_ref[k, :rows] += sums[k]
                    return carry

                lax.fori_loop(0, 9, column, 0)

        total = [jnp.sum(acc_ref[k], axis=1, keepdims=True) for k in range(4)]
        wide = jnp.where(
            lane == 0,
            total[0],
            jnp.where(lane == 1, total[1], jnp.where(lane == 2, total[2], total[3])),
        )
        flat = wide.T
        force = (place * flat[3:4] - flat[:8]) * (MU_SCALE * fix[3:4])
        emit(x, y, z, force)
        return carry

    lax.fori_loop(0, local[0] * local[1] * local[2], one_cell, 0)


def start_kernel(local, slots, occ_ref, fix_ref, pos_ref, mob_ref, speed_ref, peak_ref, *scratch):
    peak_ref[...] = jnp.zeros_like(peak_ref)

    def emit(x, y, z, force):
        mobility = mob_ref[x, y, pl.ds(z, 1)]
        speed = [mobility * force[k : k + 1] for k in range(3)]
        for k in range(3):
            speed_ref[k, x, y, pl.ds(z, 1)] = speed[k]
        square = speed[0] * speed[0] + speed[1] * speed[1] + speed[2] * speed[2]
        peak_ref[...] = jnp.maximum(peak_ref[...], square)

    sweep(local, slots, occ_ref, fix_ref, pos_ref, *scratch, emit)


def end_kernel(
    local, slots, occ_ref, step_ref, fix_ref, pos_ref, mob_ref, own_ref, speed_ref,
    moved_ref, end_ref, *scratch
):
    half = 0.5 * step_ref[0]

    def emit(x, y, z, force):
        mobility = mob_ref[x, y, pl.ds(z, 1)]
        for k in range(3):
            at = (k, x, y, pl.ds(z, 1))
            end_ref[at] = force[k : k + 1]
            moved_ref[at] = own_ref[at] + half * (speed_ref[at] + mobility * force[k : k + 1])

    sweep(local, slots, occ_ref, fix_ref, pos_ref, *scratch, emit)


def on_device(positions, line_vectors, burgers, mobility, occupancy):
    local, slots = mobility.shape[:3], mobility.shape[3]
    ext = tuple(n + 2 for n in local)
    smem = pl.BlockSpec(memory_space=pltpu.SMEM)
    vmem = pl.BlockSpec(memory_space=pltpu.VMEM)
    scratch = [
        pltpu.VMEM(ext + (128, slots), jnp.bfloat16),
        pltpu.VMEM(ext + (8, slots), jnp.float32),
        pltpu.VMEM((2, slots, 128), jnp.bfloat16),
        pltpu.VMEM((4, slots, slots), jnp.float32),
    ]
    params = pltpu.CompilerParams(vmem_limit_bytes=48 << 20)
    field = jax.ShapeDtypeStruct((3,) + mobility.shape, jnp.float32)

    lane = lax.broadcasted_iota(jnp.int32, mobility.shape, 3)
    live = (lane < occupancy[..., None]).astype(jnp.float32)
    zero = jnp.zeros_like(live)
    fix = jnp.stack(list(line_vectors) + [live] + list(burgers) + [zero], axis=3)
    rows = lambda p: jnp.stack(list(p) + [zero] * 5, axis=3)
    fix = extended(fix)
    speed, peaks = pl.pallas_call(
        functools.partial(start_kernel, local, slots),
        out_shape=(field, jax.ShapeDtypeStruct((1, slots), jnp.float32)),
        in_specs=[smem, vmem, vmem, vmem],
        out_specs=(vmem, vmem),
        scratch_shapes=scratch,
        compiler_params=params,
    )(occupancy, fix, extended(rows(positions)), mobility)
    peak = lax.pmax(jnp.max(peaks), AXES)
    step = STEP_LIMIT * lax.rsqrt(peak + 1e-12)
    predicted = positions + step * speed
    return tuple(
        pl.pallas_call(
            functools.partial(end_kernel, local, slots),
            out_shape=(field, field),
            in_specs=[smem, smem, vmem, vmem, vmem, vmem, vmem],
            out_specs=(vmem, vmem),
            scratch_shapes=scratch,
            compiler_params=params,
        )(occupancy, step[None], fix, extended(rows(predicted)), mobility, positions, speed)
    )


def solution(mesh):
    return jax.shard_map(
        on_device,
        mesh=mesh,
        in_specs=(
            P(None, "gx", "gy", "gz", None),
            P(None, "gx", "gy", "gz", None),
            P(None, "gx", "gy", "gz", None),
            P("gx", "gy", "gz", None),
            P("gx", "gy", "gz"),
        ),
        out_specs=(P(None, "gx", "gy", "gz", None), P(None, "gx", "gy", "gz", None)),
        check_vma=False,
    )
```

time: 352 us -> 246 us (0.70)
  other arithmetic: 233 us -> 0.95 us
  Pallas kernels: 0 us -> 154 us
  local copies, waits for them, and re-layouts: 43.6 us -> 2.17 us
  starting transfers between devices: 17.4 us -> 25.1 us
    reduce_sum x17 -> x0, other arithmetic: 180 us -> none  [the longest x16 180 us: tile_force(): jnp.sum(weight * separate[k], axis=-1)]
    pallas_call x0 -> x2, Pallas kernels: none -> 154 us  [the longest x1 77.3 us: on_device(): pl.pallas_call(functools.partial(end_kernel, local, slots), out_shape=(fi...]
    unnamed x52 -> x0, other arithmetic: 40.2 us -> none
    reshape x4 -> x0, local copies, waits for them, and re-layouts: 22.8 us -> none  [local_forces(): sources.reshape(width, blocks, CELL_BLOCK, sources.shape[4])]
    mul x16 -> x0, local copies, waits for them, and re-layouts: 17.9 us -> none  [inner_pairs(): left[k][..., :, None] * right[k][..., None, :]]
    ppermute x12 -> x18, starting transfers between devices: 17.4 us -> 25.1 us  [the longest x9 12.9 us: extended(): high = lax.ppermute(lax.slice_in_dim(block, 0, 1, axis=dim), axis, backward)]
    concatenate x6, other arithmetic: 3.74 us -> 0.2 us  [extended(): block = jnp.concatenate([low, block, high], axis=dim)]
    ppermute x12 -> x18, waiting for transfers between devices: 13.4 us -> 16.4 us  [the longest x9 10 us: extended(): lax.ppermute(lax.slice_in_dim(block, block.shape[dim] - 1, None, axis=dim...]
  transfers between devices with their start and end apart: 12 -> 18, of which waited for: 11 -> 13; matrix products, arithmetic and copies ran while one was open for 1% -> 0% of each run, Pallas kernels for 0% -> 0%
where the time goes in v1:
time: 246 us; the launch traced here: 242 us
  Pallas kernels  154 us (63%)
  blocking collectives  41.5 us (17%)
  starting transfers between devices  25.1 us (10%)
  waiting for transfers between devices  16.4 us (7%)
    pallas_call x1, Pallas kernels, on_device(): pl.pallas_call(functools.partial(end_kernel, local, slots), out_shape=(fi...  77.3 us
    pallas_call x1, Pallas kernels, on_device(): pl.pallas_call(functools.partial(start_kernel, local, slots), out_shape=(...  76.7 us
    pmax x1, blocking collectives, on_device(): peak = lax.pmax(jnp.max(peaks), AXES)  41.5 us
    ppermute x9, starting transfers between devices, extended(): high = lax.ppermute(lax.slice_in_dim(block, 0, 1, axis=dim), axis, backward)  12.9 us
    ppermute x9, starting transfers between devices, extended(): lax.ppermute(lax.slice_in_dim(block, block.shape[dim] - 1, None, axis=dim...  12.2 us
    ppermute x9, waiting for transfers between devices, extended(): lax.ppermute(lax.slice_in_dim(block, block.shape[dim] - 1, None, axis=dim...  10 us
    ppermute x9, waiting for transfers between devices, extended(): high = lax.ppermute(lax.slice_in_dim(block, 0, 1, axis=dim), axis, backward)  6.35 us
  transfers between devices with their start and end apart: 18, of which 13 were waited for; matrix products, arithmetic and copies ran while one was open for 0% of the time, Pallas kernels for 0%

profile of v1, /device:TPU:0, one launch (start us, length us, event | category | flops | bytes accessed | tf_op | source)
XLA Modules:
  0.0 241.7 jit_solution(16109401893246250230)
XLA Ops:
  0.6 0.8 copy.11.occ_ref
  1.4 0.1 compare_convert_fusion
  1.5 0.0 copy-start.2
  1.5 0.8 fusion.9
  2.3 0.0 copy-done.2
  2.3 0.2 stack.10
  2.6 0.0 copy-start
  2.6 3.1 %collective-permute-start = (f32[1,4,2,8,128]{4,3,2,1,0:T(8,128)S(1)}, f32[1,4,2,8,128]{4,3,2,1,0:T(8,128)S(1)}, u32[]{:S(2)}, u32[]{:S(2)}) collective-permute-start(f32[1,4,2,8,128]{4,3,2,1,0:T(8,128)S(1)} %get-tuple-element.22), channel_id=1, source_target_pairs={{0,8},{8,16},{16,24},{24,0},{1,9},{9,17},{17,25},{25,1},{2,10},{10... | collective-permute-start | bytes 98312 | tf_op jit(solution)/shard_map/ppermute | solution.py:23
  5.7 2.1 collective-permute-start.1
  7.8 0.0 copy-done
  7.8 0.1 stack.11
  7.9 0.1 collective-permute-start.6
  8.0 3.8 %collective-permute-start.7 = (f32[1,4,2,8,128]{4,3,2,1,0:T(8,128)S(1)}, f32[1,4,2,8,128]{4,3,2,1,0:T(8,128)S(1)}, u32[]{:S(2)}, u32[]{:S(2)}) collective-permute-start(f32[1,4,2,8,128]{4,3,2,1,0:T(8,128)S(1)} %get-tuple-element.21), channel_id=1, source_target_pairs={{8,0},{16,8},{24,16},{0,24},{9,1},{17,9},{25,17},{1,25},{10,2},{18... | collective-permute-start | bytes 98312 | tf_op jit(solution)/shard_map/ppermute | solution.py:26
  11.8 0.0 collective-permute-done
  11.8 0.0 collective-permute-done.1
  11.8 1.7 collective-permute-start.2
  13.6 0.3 collective-permute-start.3
  13.9 0.0 collective-permute-done.6
  13.9 0.0 collective-permute-done.7
  14.0 1.7 collective-permute-start.8
  15.7 0.3 collective-permute-start.9
  16.0 0.3 collective-permute-done.2
  16.3 1.3 collective-permute-done.3
  17.7 0.1 collective-permute-start.4
  17.8 1.7 collective-permute-start.5
  19.5 0.0 collective-permute-done.8
  19.5 0.3 collective-permute-done.9
  19.8 0.1 collective-permute-start.10
  19.9 1.7 collective-permute-start.11
  21.6 0.7 collective-permute-done.4
  22.3 1.4 collective-permute-done.5
  23.8 0.0 copy-start.1
  23.8 2.2 collective-permute-done.10
  26.0 0.1 collective-permute-done.11
  26.2 0.0 copy-done.1
  26.2 76.7 %shard_map.68 = (f32[3,4,4,2,128]{4,3,2,1,0:T(2,128)S(1)}, f32[1,128]{1,0:T(1,128)S(1)}) custom-call(s32[4,4,2]{2,1,0:T(4,128)S(1)} %copy.11.occ_ref, f32[6,6,4,8,128]{4,3,2,1,0:T(8,128)S(1)} %pad_maximum_fusion.fix_ref, f32[6,6,4,8,128]{4,3,2,1,0:T(8,128)S(1)} %pad_maximum_fusion.1.pos_ref, f32[4,4,2,128]{3,2,1,0:T(2,128)S(1)} %copy-done.1), custom_call_target="tpu_custom_call" | custom-call | tf_op jit(solution)/shard_map/pallas_call | solution.py:197
  102.9 0.6 reduce_max.9
  103.5 41.5 %pmax.7 = f32[]{:T(128)} all-reduce(f32[]{:T(128)} %reduce_max.9), channel_id=1, replica_groups=mesh['gx'=4,'gy'=2,'gz'=4] {'gx','gy','gz'}, use_global_device_ids=true, to_apply=%region_1.0 | all-reduce | flops 1 | bytes 8 | tf_op jit(solution)/shard_map/pmax | solution.py:205
  145.7 0.1 stack.12
  145.9 2.9 %collective-permute-start.12 = (f32[1,4,2,8,128]{4,3,2,1,0:T(8,128)S(1)}, f32[1,4,2,8,128]{4,3,2,1,0:T(8,128)S(1)}, u32[]{:S(2)}, u32[]{:S(2)}) collective-permute-start(f32[1,4,2,8,128]{4,3,2,1,0:T(8,128)S(1)} %get-tuple-element.18), channel_id=1, source_target_pairs={{0,8},{8,16},{16,24},{24,0},{1,9},{9,17},{17,25},{25,1},{2,10},{10... | collective-permute-start | bytes 98312 | tf_op jit(solution)/shard_map/ppermute | solution.py:23
  148.8 1.0 collective-permute-start.13
  149.8 1.9 collective-permute-done.12
  151.7 1.0 collective-permute-done.13
  152.7 2.5 %collective-permute-start.14 = (f32[6,1,2,8,128]{4,3,2,1,0:T(8,128)S(1)}, f32[6,1,2,8,128]{4,3,2,1,0:T(8,128)S(1)}, u32[]{:S(2)}, u32[]{:S(2)}) collective-permute-start(f32[6,1,2,8,128]{4,3,2,1,0:T(8,128)S(1)} %get-tuple-element.12), channel_id=1, source_target_pairs={{0,4},{4,0},{1,5},{5,1},{2,6},{6,2},{3,7},{7,3},{8,12},{12,8},{9,1... | collective-permute-start | bytes 147464 | tf_op jit(solution)/shard_map/ppermute | solution.py:23
  155.2 0.1 collective-permute-start.15
  155.3 2.0 collective-permute-done.14
  157.3 2.0 collective-permute-done.15
  159.4 0.1 collective-permute-start.16
  159.4 1.7 collective-permute-start.17
  161.2 2.9 %collective-permute-done.16 = f32[6,6,1,8,128]{4,3,2,1,0:T(8,128)S(1)} collective-permute-done((f32[6,6,1,8,128]{4,3,2,1,0:T(8,128)S(1)}, f32[6,6,1,8,128]{4,3,2,1,0:T(8,128)S(1)}, u32[]{:S(2)}, u32[]{:S(2)}) %collective-permute-start.16) | collective-permute-done | bytes 147488 | tf_op jit(solution)/shard_map/ppermute | solution.py:23
  164.1 0.2 collective-permute-done.17
  164.4 77.3 %shard_map.69 = (f32[3,4,4,2,128]{4,3,2,1,0:T(2,128)}, f32[3,4,4,2,128]{4,3,2,1,0:T(2,128)}) custom-call(s32[4,4,2]{2,1,0:T(4,128)S(1)} %copy.11.occ_ref, f32[1]{0:T(128)} %bitcast.9.step_ref, f32[6,6,4,8,128]{4,3,2,1,0:T(8,128)S(1)} %pad_maximum_fusion.fix_ref, f32[6,6,4,8,128]{4,3,2,1,0:T(8,128)S(1)} %pad_maximum_fusion.2.pos_ref, ...), custom_call_target="tpu_custom_call" | custom-call | tf_op jit(solution)/shard_map/pallas_call | solution.py:209
  (21 shorter events, 0.4 us)
Async XLA Ops:
  1.5 0.8 copy-start.2
  2.6 5.2 %copy-start = (f32[3,4,4,2,128]{4,3,2,1,0:T(2,128)S(1)}, f32[3,4,4,2,128]{4,3,2,1,0:T(2,128)}, u32[]{:S(2)}) copy-start(f32[3,4,4,2,128]{4,3,2,1,0:T(2,128)} %own_ref.1) | copy-start | bytes 147460
  2.6 9.2 %collective-permute-start = (f32[1,4,2,8,128]{4,3,2,1,0:T(8,128)S(1)}, f32[1,4,2,8,128]{4,3,2,1,0:T(8,128)S(1)}, u32[]{:S(2)}, u32[]{:S(2)}) collective-permute-start(f32[1,4,2,8,128]{4,3,2,1,0:T(8,128)S(1)} %get-tuple-element.22), channel_id=1, source_target_pairs={{0,8},{8,16},{16,24},{24,0},{1,9},{9,17},{17,25},{25,1},{2,10},{10... | collective-permute-start | bytes 98312 | tf_op jit(solution)/shard_map/ppermute | solution.py:23
  5.7 6.1 %collective-permute-start.1 = (f32[1,4,2,8,128]{4,3,2,1,0:T(8,128)S(1)}, f32[1,4,2,8,128]{4,3,2,1,0:T(8,128)S(1)}, u32[]{:S(2)}, u32[]{:S(2)}) collective-permute-start(f32[1,4,2,8,128]{4,3,2,1,0:T(8,128)S(1)} %get-tuple-element.23), channel_id=1, source_target_pairs={{8,0},{16,8},{24,16},{0,24},{9,1},{17,9},{25,17},{1,25},{10,2},{18... | collective-permute-start | bytes 98312 | tf_op jit(solution)/shard_map/ppermute | solution.py:26
  7.9 6.0 %collective-permute-start.6 = (f32[1,4,2,8,128]{4,3,2,1,0:T(8,128)S(1)}, f32[1,4,2,8,128]{4,3,2,1,0:T(8,128)S(1)}, u32[]{:S(2)}, u32[]{:S(2)}) collective-permute-start(f32[1,4,2,8,128]{4,3,2,1,0:T(8,128)S(1)} %get-tuple-element.20), channel_id=1, source_target_pairs={{0,8},{8,16},{16,24},{24,0},{1,9},{9,17},{17,25},{25,1},{2,10},{10... | collective-permute-start | bytes 98312 | tf_op jit(solution)/shard_map/ppermute | solution.py:23
  8.0 5.9 %collective-permute-start.7 = (f32[1,4,2,8,128]{4,3,2,1,0:T(8,128)S(1)}, f32[1,4,2,8,128]{4,3,2,1,0:T(8,128)S(1)}, u32[]{:S(2)}, u32[]{:S(2)}) collective-permute-start(f32[1,4,2,8,128]{4,3,2,1,0:T(8,128)S(1)} %get-tuple-element.21), channel_id=1, source_target_pairs={{8,0},{16,8},{24,16},{0,24},{9,1},{17,9},{25,17},{1,25},{10,2},{18... | collective-permute-start | bytes 98312 | tf_op jit(solution)/shard_map/ppermute | solution.py:26
  11.8 4.5 %collective-permute-start.2 = (f32[6,1,2,8,128]{4,3,2,1,0:T(8,128)S(1)}, f32[6,1,2,8,128]{4,3,2,1,0:T(8,128)S(1)}, u32[]{:S(2)}, u32[]{:S(2)}) collective-permute-start(f32[6,1,2,8,128]{4,3,2,1,0:T(8,128)S(1)} %get-tuple-element.16), channel_id=1, source_target_pairs={{0,4},{4,0},{1,5},{5,1},{2,6},{6,2},{3,7},{7,3},{8,12},{12,8},{9,1... | collective-permute-start | bytes 147464 | tf_op jit(solution)/shard_map/ppermute | solution.py:23
  13.6 4.1 %collective-permute-start.3 = (f32[6,1,2,8,128]{4,3,2,1,0:T(8,128)S(1)}, f32[6,1,2,8,128]{4,3,2,1,0:T(8,128)S(1)}, u32[]{:S(2)}, u32[]{:S(2)}) collective-permute-start(f32[6,1,2,8,128]{4,3,2,1,0:T(8,128)S(1)} %get-tuple-element.17), channel_id=1, source_target_pairs={{4,0},{0,4},{5,1},{1,5},{6,2},{2,6},{7,3},{3,7},{12,8},{8,12},{13,... | collective-permute-start | bytes 147464 | tf_op jit(solution)/shard_map/ppermute | solution.py:26
  14.0 5.6 %collective-permute-start.8 = (f32[6,1,2,8,128]{4,3,2,1,0:T(8,128)S(1)}, f32[6,1,2,8,128]{4,3,2,1,0:T(8,128)S(1)}, u32[]{:S(2)}, u32[]{:S(2)}) collective-permute-start(f32[6,1,2,8,128]{4,3,2,1,0:T(8,128)S(1)} %get-tuple-element.14), channel_id=1, source_target_pairs={{0,4},{4,0},{1,5},{5,1},{2,6},{6,2},{3,7},{7,3},{8,12},{12,8},{9,1... | collective-permute-start | bytes 147464 | tf_op jit(solution)/shard_map/ppermute | solution.py:23
  15.7 4.1 %collective-permute-start.9 = (f32[6,1,2,8,128]{4,3,2,1,0:T(8,128)S(1)}, f32[6,1,2,8,128]{4,3,2,1,0:T(8,128)S(1)}, u32[]{:S(2)}, u32[]{:S(2)}) collective-permute-start(f32[6,1,2,8,128]{4,3,2,1,0:T(8,128)S(1)} %get-tuple-element.15), channel_id=1, source_target_pairs={{4,0},{0,4},{5,1},{1,5},{6,2},{2,6},{7,3},{3,7},{12,8},{8,12},{13,... | collective-permute-start | bytes 147464 | tf_op jit(solution)/shard_map/ppermute | solution.py:26
  17.7 4.6 %collective-permute-start.4 = (f32[6,6,1,8,128]{4,3,2,1,0:T(8,128)S(1)}, f32[6,6,1,8,128]{4,3,2,1,0:T(8,128)S(1)}, u32[]{:S(2)}, u32[]{:S(2)}) collective-permute-start(f32[6,6,1,8,128]{4,3,2,1,0:T(8,128)S(1)} %get-tuple-element.10), channel_id=1, source_target_pairs={{0,1},{1,2},{2,3},{3,0},{4,5},{5,6},{6,7},{7,4},{8,9},{9,10},{10,1... | collective-permute-start | bytes 442376 | tf_op jit(solution)/shard_map/ppermute | solution.py:23
  17.8 6.0 %collective-permute-start.5 = (f32[6,6,1,8,128]{4,3,2,1,0:T(8,128)S(1)}, f32[6,6,1,8,128]{4,3,2,1,0:T(8,128)S(1)}, u32[]{:S(2)}, u32[]{:S(2)}) collective-permute-start(f32[6,6,1,8,128]{4,3,2,1,0:T(8,128)S(1)} %get-tuple-element.11), channel_id=1, source_target_pairs={{1,0},{2,1},{3,2},{0,3},{5,4},{6,5},{7,6},{4,7},{9,8},{10,9},{11,1... | collective-permute-start | bytes 442376 | tf_op jit(solution)/shard_map/ppermute | solution.py:26
  19.8 6.2 %collective-permute-start.10 = (f32[6,6,1,8,128]{4,3,2,1,0:T(8,128)S(1)}, f32[6,6,1,8,128]{4,3,2,1,0:T(8,128)S(1)}, u32[]{:S(2)}, u32[]{:S(2)}) collective-permute-start(f32[6,6,1,8,128]{4,3,2,1,0:T(8,128)S(1)} %get-tuple-element.8), channel_id=1, source_target_pairs={{0,1},{1,2},{2,3},{3,0},{4,5},{5,6},{6,7},{7,4},{8,9},{9,10},{10,1... | collective-permute-start | bytes 442376 | tf_op jit(solution)/shard_map/ppermute | solution.py:23
  19.9 6.2 %collective-permute-start.11 = (f32[6,6,1,8,128]{4,3,2,1,0:T(8,128)S(1)}, f32[6,6,1,8,128]{4,3,2,1,0:T(8,128)S(1)}, u32[]{:S(2)}, u32[]{:S(2)}) collective-permute-start(f32[6,6,1,8,128]{4,3,2,1,0:T(8,128)S(1)} %get-tuple-element.9), channel_id=1, source_target_pairs={{1,0},{2,1},{3,2},{0,3},{5,4},{6,5},{7,6},{4,7},{9,8},{10,9},{11,1... | collective-permute-start | bytes 442376 | tf_op jit(solution)/shard_map/ppermute | solution.py:26
  23.8 2.3 copy-start.1
  145.9 5.8 %collective-permute-start.12 = (f32[1,4,2,8,128]{4,3,2,1,0:T(8,128)S(1)}, f32[1,4,2,8,128]{4,3,2,1,0:T(8,128)S(1)}, u32[]{:S(2)}, u32[]{:S(2)}) collective-permute-start(f32[1,4,2,8,128]{4,3,2,1,0:T(8,128)S(1)} %get-tuple-element.18), channel_id=1, source_target_pairs={{0,8},{8,16},{16,24},{24,0},{1,9},{9,17},{17,25},{25,1},{2,10},{10... | collective-permute-start | bytes 98312 | tf_op jit(solution)/shard_map/ppermute | solution.py:23
  148.8 3.9 %collective-permute-start.13 = (f32[1,4,2,8,128]{4,3,2,1,0:T(8,128)S(1)}, f32[1,4,2,8,128]{4,3,2,1,0:T(8,128)S(1)}, u32[]{:S(2)}, u32[]{:S(2)}) collective-permute-start(f32[1,4,2,8,128]{4,3,2,1,0:T(8,128)S(1)} %get-tuple-element.19), channel_id=1, source_target_pairs={{8,0},{16,8},{24,16},{0,24},{9,1},{17,9},{25,17},{1,25},{10,2},{18... | collective-permute-start | bytes 98312 | tf_op jit(solution)/shard_map/ppermute | solution.py:26
  152.7 4.6 %collective-permute-start.14 = (f32[6,1,2,8,128]{4,3,2,1,0:T(8,128)S(1)}, f32[6,1,2,8,128]{4,3,2,1,0:T(8,128)S(1)}, u32[]{:S(2)}, u32[]{:S(2)}) collective-permute-start(f32[6,1,2,8,128]{4,3,2,1,0:T(8,128)S(1)} %get-tuple-element.12), channel_id=1, source_target_pairs={{0,4},{4,0},{1,5},{5,1},{2,6},{6,2},{3,7},{7,3},{8,12},{12,8},{9,1... | collective-permute-start | bytes 147464 | tf_op jit(solution)/shard_map/ppermute | solution.py:23
  155.2 4.1 %collective-permute-start.15 = (f32[6,1,2,8,128]{4,3,2,1,0:T(8,128)S(1)}, f32[6,1,2,8,128]{4,3,2,1,0:T(8,128)S(1)}, u32[]{:S(2)}, u32[]{:S(2)}) collective-permute-start(f32[6,1,2,8,128]{4,3,2,1,0:T(8,128)S(1)} %get-tuple-element.13), channel_id=1, source_target_pairs={{4,0},{0,4},{5,1},{1,5},{6,2},{2,6},{7,3},{3,7},{12,8},{8,12},{13,... | collective-permute-start | bytes 147464 | tf_op jit(solution)/shard_map/ppermute | solution.py:26
  159.4 4.7 %collective-permute-start.16 = (f32[6,6,1,8,128]{4,3,2,1,0:T(8,128)S(1)}, f32[6,6,1,8,128]{4,3,2,1,0:T(8,128)S(1)}, u32[]{:S(2)}, u32[]{:S(2)}) collective-permute-start(f32[6,6,1,8,128]{4,3,2,1,0:T(8,128)S(1)} %get-tuple-element.6), channel_id=1, source_target_pairs={{0,1},{1,2},{2,3},{3,0},{4,5},{5,6},{6,7},{7,4},{8,9},{9,10},{10,1... | collective-permute-start | bytes 442376 | tf_op jit(solution)/shard_map/ppermute | solution.py:23
  159.4 4.9 %collective-permute-start.17 = (f32[6,6,1,8,128]{4,3,2,1,0:T(8,128)S(1)}, f32[6,6,1,8,128]{4,3,2,1,0:T(8,128)S(1)}, u32[]{:S(2)}, u32[]{:S(2)}) collective-permute-start(f32[6,6,1,8,128]{4,3,2,1,0:T(8,128)S(1)} %get-tuple-element.7), channel_id=1, source_target_pairs={{1,0},{2,1},{3,2},{0,3},{5,4},{6,5},{7,6},{4,7},{9,8},{10,9},{11,1... | collective-permute-start | bytes 442376 | tf_op jit(solution)/shard_map/ppermute | solution.py:26

commit v2 on v1

--- a/solution.py
+++ b/solution.py
@@ -1,4 +1,5 @@
 import functools
+import itertools
 
 import jax
 import jax.numpy as jnp
@@ -15,17 +16,86 @@
 K_ROWS = 72
 
 
-def extended(block):
-    for dim, axis in enumerate(AXES):
-        count = lax.axis_size(axis)
-        forward = [(i, (i + 1) % count) for i in range(count)]
-        backward = [(target, source) for source, target in forward]
-        low = lax.ppermute(
-            lax.slice_in_dim(block, block.shape[dim] - 1, None, axis=dim), axis, forward
+def peers(shape):
+    spans = [range(n) for n in shape]
+    return [o for o in itertools.product(*spans) if any(o)]
+
+
+def device_at(offset, shape):
+    return tuple(
+        lax.rem(lax.axis_index(a) + (o % n), n) for a, o, n in zip(AXES, offset, shape)
+    )
+
+
+def halo_messages(shape, local, block, padded):
+    for shift in itertools.product((-1, 0, 1), repeat=3):
+        if any(shift):
+            take = tuple({-1: pl.ds(0, 1), 0: pl.ds(0, n), 1: pl.ds(n - 1, 1)}[s] for s, n in zip(shift, local))
+            put = tuple({-1: pl.ds(n + 1, 1), 0: pl.ds(1, n), 1: pl.ds(0, 1)}[s] for s, n in zip(shift, local))
+            yield device_at(shift, shape), block.at[take], padded.at[put]
+
+
+def exchange(shape, local, blocks, padded, extra, greet, send_sem, recv_sem, own_sem):
+    barrier = pltpu.get_barrier_semaphore()
+    for offset in greet:
+        pl.semaphore_signal(
+            barrier, inc=1, device_id=device_at(offset, shape), device_id_type=pl.DeviceIdType.MESH
         )
-        high = lax.ppermute(lax.slice_in_dim(block, 0, 1, axis=dim), axis, backward)
-        block = jnp.concatenate([low, block, high], axis=dim)
-    return block
+    inner = tuple(pl.ds(1, n) for n in local)
+    own = [
+        pltpu.make_async_copy(b, p.at[inner], own_sem.at[i])
+        for i, (b, p) in enumerate(zip(blocks, padded))
+    ]
+    for copy in own:
+        copy.start()
+    messages = list(extra)
+    for b, p in zip(blocks, padded):
+        messages += list(halo_messages(shape, local, b, p))
+    pl.semaphore_wait(barrier, len(greet))
+    copies = [
+        pltpu.make_async_remote_copy(
+            src_ref=source,
+            dst_ref=target,
+            send_sem=send_sem.at[i],
+            recv_sem=recv_sem.at[i],
+            device_id=device,
+            device_id_type=pl.DeviceIdType.MESH,
+        )
+        for i, (device, source, target) in enumerate(messages)
+    ]
+    for copy in copies:
+        copy.start()
+    for copy in copies + own:
+        copy.wait()
+
+
+def fixed_halo_kernel(shape, local, fix_ref, rest_ref, fix_out, rest_out, *sems):
+    near = [s for s in itertools.product((-1, 0, 1), repeat=3) if any(s)]
+    exchange(shape, local, (fix_ref, rest_ref), (fix_out, rest_out), [], near, *sems)
+
+
+def speed_halo_kernel(shape, local, speed_ref, peak_ref, speed_out, peaks_out, *sems):
+    others = peers(shape)
+    extra = [
+        (device_at(o, shape), peak_ref, peaks_out.at[i]) for i, o in enumerate(others)
+    ]
+    exchange(shape, local, (speed_ref,), (speed_out,), extra, others, *sems)
+
+
+def halo_call(kernel, out_shape, messages, collective, *args):
+    vmem = pl.BlockSpec(memory_space=pltpu.VMEM)
+    return pl.pallas_call(
+        kernel,
+        out_shape=out_shape,
+        in_specs=[vmem] * len(args),
+        out_specs=tuple(vmem for _ in out_shape),
+        scratch_shapes=[
+            pltpu.SemaphoreType.DMA((messages,)),
+            pltpu.SemaphoreType.DMA((messages,)),
+            pltpu.SemaphoreType.DMA((2,)),
+        ],
+        compiler_params=pltpu.CompilerParams(collective_id=collective, has_side_effects=True),
+    )(*args)
 
 
 def split(value, parts):
@@ -75,7 +145,7 @@
     return jnp.concatenate(high + high + low + [h, h, m, m, h, l, zero], axis=0)
 
 
-def sweep(local, slots, occ_ref, fix_ref, pos_ref, base_ref, place_ref, lhs_ref, acc_ref, emit):
+def sweep(local, slots, occ_ref, fix_ref, spot, base_ref, place_ref, lhs_ref, acc_ref, emit):
     ext = tuple(n + 2 for n in local)
     row = lax.broadcasted_iota(jnp.int32, (8, slots), 0)
 
@@ -83,7 +153,7 @@
         z = lax.rem(c, ext[2])
         y = lax.rem(c // ext[2], ext[1])
         x = c // (ext[2] * ext[1])
-        place = jnp.where(row < 3, pos_ref[x, y, z] + offsets(row, (x, y, z), local), 0.0)
+        place = jnp.where(row < 3, spot(x, y, z) + offsets(row, (x, y, z), local), 0.0)
         place_ref[x, y, z] = place
         base_ref[x, y, z] = source_rows(fix_ref[x, y, z], place, row).astype(jnp.bfloat16)
         return carry
@@ -110,25 +180,20 @@
                 rows = 32 * group
                 lhs = jnp.concatenate([lhs_ref[0, :rows], lhs_ref[1, :rows]], axis=0)
 
-                def column(i, carry):
-                    sx = x + i // 3
-                    sy = y + lax.rem(i, 3)
-                    rhs = jnp.concatenate([base_ref[sx, sy, z + d] for d in range(3)], axis=1)
+                for i, j in itertools.product(range(3), repeat=2):
+                    near = [(x + i, y + j, z + d) for d in range(3)]
+                    rhs = jnp.concatenate([base_ref[at] for at in near], axis=1)
                     both = jnp.dot(lhs, rhs, preferred_element_type=jnp.float32)
                     inverse = lax.rsqrt(both[rows:])
                     weight = both[:rows] * (inverse * inverse * inverse)
                     sums = [0.0] * 4
-                    for d in range(3):
+                    for d, at in enumerate(near):
                         part = weight[:, d * slots : (d + 1) * slots]
                         sums[3] = sums[3] + part
                         for k in range(3):
-                            coord = place_ref[sx, sy, z + d, k : k + 1]
-                            sums[k] = sums[k] + part * coord
+                            sums[k] = sums[k] + part * place_ref[at + (pl.ds(k, 1),)]
                     for k in range(4):
                         acc_ref[k, :rows] += sums[k]
-                    return carry
-
-                lax.fori_loop(0, 9, column, 0)
 
         total = [jnp.sum(acc_ref[k], axis=1, keepdims=True) for k in range(4)]
         wide = jnp.where(
@@ -144,37 +209,52 @@
     lax.fori_loop(0, local[0] * local[1] * local[2], one_cell, 0)
 
 
-def start_kernel(local, slots, occ_ref, fix_ref, pos_ref, mob_ref, speed_ref, peak_ref, *scratch):
+def stacked(parts):
+    fill = jnp.zeros((8 - sum(p.shape[0] for p in parts),) + parts[0].shape[1:], jnp.float32)
+    return jnp.concatenate(list(parts) + [fill], axis=0)
+
+
+def start_kernel(local, slots, occ_ref, fix_ref, rest_ref, mob_ref, speed_ref, peak_ref, *scratch):
     peak_ref[...] = jnp.zeros_like(peak_ref)
+
+    def spot(x, y, z):
+        return stacked([fix_ref[x, y, z, 7:8], rest_ref[x, y, z]])
+
+    def emit(x, y, z, force):
+        speed = mob_ref[x, y, pl.ds(z, 1)] * force
+        speed_ref[x, y, z] = speed[:4]
+        square = speed[0:1] * speed[0:1] + speed[1:2] * speed[1:2] + speed[2:3] * speed[2:3]
+        peak_ref[...] = jnp.maximum(peak_ref[...], square)
+
+    sweep(local, slots, occ_ref, fix_ref, spot, *scratch, emit)
+
+
+def end_kernel(
+    local, slots, occ_ref, fix_ref, rest_ref, mob_ref, own_ref, speed_ref, peak_ref, peaks_ref,
+    moved_ref, end_ref, *scratch
+):
+    peak = jnp.maximum(peak_ref[...], jnp.max(peaks_ref[...], axis=0))
+    peak = jnp.max(peak, axis=1, keepdims=True)
+    step = STEP_LIMIT * lax.rsqrt(peak + 1e-12)
+
+    def spot(x, y, z):
+        place = stacked([fix_ref[x, y, z, 7:8], rest_ref[x, y, z]])
+        return place + step * stacked([speed_ref[x, y, z]])
 
     def emit(x, y, z, force):
         mobility = mob_ref[x, y, pl.ds(z, 1)]
-        speed = [mobility * force[k : k + 1] for k in range(3)]
-        for k in range(3):
-            speed_ref[k, x, y, pl.ds(z, 1)] = speed[k]
-        square = speed[0] * speed[0] + speed[1] * speed[1] + speed[2] * speed[2]
-        peak_ref[...] = jnp.maximum(peak_ref[...], square)
-
-    sweep(local, slots, occ_ref, fix_ref, pos_ref, *scratch, emit)
-
-
-def end_kernel(
-    local, slots, occ_ref, step_ref, fix_ref, pos_ref, mob_ref, own_ref, speed_ref,
-    moved_ref, end_ref, *scratch
-):
-    half = 0.5 * step_ref[0]
-
-    def emit(x, y, z, force):
-        mobility = mob_ref[x, y, pl.ds(z, 1)]
+        speed = speed_ref[x + 1, y + 1, z + 1]
         for k in range(3):
             at = (k, x, y, pl.ds(z, 1))
             end_ref[at] = force[k : k + 1]
-            moved_ref[at] = own_ref[at] + half * (speed_ref[at] + mobility * force[k : k + 1])
-
-    sweep(local, slots, occ_ref, fix_ref, pos_ref, *scratch, emit)
-
-
-def on_device(positions, line_vectors, burgers, mobility, occupancy):
+            moved_ref[at] = own_ref[at] + (0.5 * step) * (
+                speed[k : k + 1] + mobility * force[k : k + 1]
+            )
+
+    sweep(local, slots, occ_ref, fix_ref, spot, *scratch, emit)
+
+
+def on_device(shape, positions, line_vectors, burgers, mobility, occupancy):
     local, slots = mobility.shape[:3], mobility.shape[3]
     ext = tuple(n + 2 for n in local)
     smem = pl.BlockSpec(memory_space=pltpu.SMEM)
@@ -186,40 +266,53 @@
         pltpu.VMEM((4, slots, slots), jnp.float32),
     ]
     params = pltpu.CompilerParams(vmem_limit_bytes=48 << 20)
+    rows = lambda lead, n: jax.ShapeDtypeStruct(lead + (n, slots), jnp.float32)
     field = jax.ShapeDtypeStruct((3,) + mobility.shape, jnp.float32)
+    others = len(peers(shape))
 
     lane = lax.broadcasted_iota(jnp.int32, mobility.shape, 3)
     live = (lane < occupancy[..., None]).astype(jnp.float32)
-    zero = jnp.zeros_like(live)
-    fix = jnp.stack(list(line_vectors) + [live] + list(burgers) + [zero], axis=3)
-    rows = lambda p: jnp.stack(list(p) + [zero] * 5, axis=3)
-    fix = extended(fix)
-    speed, peaks = pl.pallas_call(
+    fix = jnp.stack(list(line_vectors) + [live] + list(burgers) + [positions[0]], axis=3)
+    rest = jnp.stack(list(positions[1:]), axis=3)
+    fix, rest = halo_call(
+        functools.partial(fixed_halo_kernel, shape, local),
+        (rows(ext, 8), rows(ext, 2)),
+        52,
+        0,
+        fix,
+        rest,
+    )
+    speed, peak = pl.pallas_call(
         functools.partial(start_kernel, local, slots),
-        out_shape=(field, jax.ShapeDtypeStruct((1, slots), jnp.float32)),
+        out_shape=(rows(local, 4), rows((), 1)),
         in_specs=[smem, vmem, vmem, vmem],
         out_specs=(vmem, vmem),
         scratch_shapes=scratch,
         compiler_params=params,
-    )(occupancy, fix, extended(rows(positions)), mobility)
-    peak = lax.pmax(jnp.max(peaks), AXES)
-    step = STEP_LIMIT * lax.rsqrt(peak + 1e-12)
-    predicted = positions + step * speed
+    )(occupancy, fix, rest, mobility)
+    speed, peaks = halo_call(
+        functools.partial(speed_halo_kernel, shape, local),
+        (rows(ext, 4), rows((others,), 1)),
+        26 + others,
+        1,
+        speed,
+        peak,
+    )
     return tuple(
         pl.pallas_call(
             functools.partial(end_kernel, local, slots),
             out_shape=(field, field),
-            in_specs=[smem, smem, vmem, vmem, vmem, vmem, vmem],
+            in_specs=[smem] + [vmem] * 7,
             out_specs=(vmem, vmem),
             scratch_shapes=scratch,
             compiler_params=params,
-        )(occupancy, step[None], fix, extended(rows(predicted)), mobility, positions, speed)
+        )(occupancy, fix, rest, mobility, positions, speed, peak, peaks)
     )
 
 
 def solution(mesh):
     return jax.shard_map(
-        on_device,
+        functools.partial(on_device, tuple(mesh.shape[a] for a in AXES)),
         mesh=mesh,
         in_specs=(
             P(None, "gx", "gy", "gz", None),

time: 246 us -> 116 us (0.47); the launches traced: 242 us -> 116 us
  Pallas kernels: 154 us -> 106 us
  blocking collectives: 41.5 us -> 0 us
  starting transfers between devices: 25.1 us -> 0 us
  waiting for transfers between devices: 16.4 us -> 0 us
  local copies, waits for them, and re-layouts: 2.17 us -> 8.64 us
    pmax x1 -> x0, blocking collectives: 41.5 us -> none  [on_device(): peak = lax.pmax(jnp.max(peaks), AXES)]
    pallas_call x1, Pallas kernels: 76.7 us -> 38.2 us  [on_device(): pl.pallas_call(functools.partial(start_kernel, local, slots), out_shape=(...]
    pallas_call x1, Pallas kernels: 77.3 us -> 39.2 us  [on_device(): pl.pallas_call(functools.partial(end_kernel, local, slots), out_shape=(fi...]
    pallas_call x0 -> x2, Pallas kernels: none -> 28.7 us  [halo_call(): pl.pallas_call(kernel, out_shape=out_shape, in_specs=[vmem] * len(args),...]
    ppermute x18 -> x0, starting transfers between devices: 25.1 us -> none  [the longest x9 12.9 us: extended(): high = lax.ppermute(lax.slice_in_dim(block, 0, 1, axis=dim), axis, backward)]
    ppermute x18 -> x0, waiting for transfers between devices: 16.4 us -> none  [the longest x9 10 us: extended(): lax.ppermute(lax.slice_in_dim(block, block.shape[dim] - 1, None, axis=dim...]
    unnamed x7 -> x25, local copies, waits for them, and re-layouts: 0.83 us -> 7.03 us
  transfers between devices with their start and end apart: 18 -> 0, of which waited for: 13 -> 0; matrix products, arithmetic and copies ran while one was open for 0% -> 0% of each run, Pallas kernels for 0% -> 0%
where the time goes in v2:
time: 116 us
  Pallas kernels  106 us (91%)
  local copies, waits for them, and re-layouts  8.64 us (7%)
    pallas_call x1, Pallas kernels, on_device(): pl.pallas_call(functools.partial(end_kernel, local, slots), out_shape=(fi...  39.2 us
    pallas_call x1, Pallas kernels, on_device(): pl.pallas_call(functools.partial(start_kernel, local, slots), out_shape=(...  38.2 us
    pallas_call x2, Pallas kernels, halo_call(): pl.pallas_call(kernel, out_shape=out_shape, in_specs=[vmem] * len(args),...  28.7 us
    unnamed x25, local copies, waits for them, and re-layouts  7.03 us

profile of v2, /device:TPU:0, one launch (start us, length us, event | category | flops | bytes accessed | tf_op | source)
XLA Modules:
  0.0 116.2 jit_solution(12034452147213911212)
XLA Ops:
  0.6 0.8 copy.9.occ_ref
  1.4 0.1 compare_convert_fusion
  1.5 0.0 copy-start.11
  1.5 0.8 fusion.2
  2.3 0.0 copy-done.11
  2.3 0.0 copy-start.5
  2.3 0.8 copy-done.5
  3.1 0.6 pad_maximum_fusion.rest_ref
  3.8 0.8 stack.7.fix_ref
  4.6 0.0 copy-start.6
  4.6 16.6 %shard_map.68 = (f32[6,6,4,8,128]{4,3,2,1,0:T(8,128)}, f32[6,6,4,2,128]{4,3,2,1,0:T(2,128)}) custom-call(f32[4,4,2,8,128]{4,3,2,1,0:T(8,128)} %stack.7.fix_ref, f32[4,4,2,2,128]{4,3,2,1,0:T(2,128)} %pad_maximum_fusion.rest_ref), custom_call_target="tpu_custom_call" | custom-call | tf_op jit(solution)/shard_map/pallas_call | solution.py:87
  21.2 0.0 copy-done.6
  21.2 0.0 copy-start
  21.2 1.1 copy-done
  22.3 0.0 copy-start.2
  22.3 0.9 copy-done.2
  23.2 0.0 copy-start.1
  23.2 0.0 copy-start.3
  23.2 38.2 %shard_map.69 = (f32[4,4,2,4,128]{4,3,2,1,0:T(4,128)S(1)}, f32[1,128]{1,0:T(1,128)S(1)}) custom-call(s32[4,4,2]{2,1,0:T(4,128)S(1)} %copy.9.occ_ref, f32[6,6,4,8,128]{4,3,2,1,0:T(8,128)S(1)} %copy-done, f32[6,6,4,2,128]{4,3,2,1,0:T(2,128)S(1)} %copy-done.2, f32[4,4,2,128]{3,2,1,0:T(2,128)S(1)} %copy-done.6), custom_call_target="tpu_custom_call" | custom-call | tf_op jit(solution)/shard_map/pallas_call | solution.py:285
  61.4 0.0 copy-start.7
  61.4 0.6 copy-done.7
  62.0 0.0 copy-start.9
  62.0 0.5 copy-done.9
  62.5 12.1 %shard_map.70 = (f32[6,6,4,4,128]{4,3,2,1,0:T(4,128)}, f32[31,1,128]{2,1,0:T(1,128)}) custom-call(f32[4,4,2,4,128]{4,3,2,1,0:T(4,128)} %copy-done.7, f32[1,128]{1,0:T(1,128)} %copy-done.9), custom_call_target="tpu_custom_call" | custom-call | tf_op jit(solution)/shard_map/pallas_call | solution.py:87
  74.7 0.0 copy-start.10
  74.7 0.0 copy-done.1
  74.7 0.0 copy-done.3
  74.7 0.6 copy-done.10
  75.3 0.0 copy-start.4
  75.3 1.0 copy-done.4
  76.3 0.0 copy-start.8
  76.3 0.7 copy-done.8
  77.0 39.2 %shard_map.71 = (f32[3,4,4,2,128]{4,3,2,1,0:T(2,128)}, f32[3,4,4,2,128]{4,3,2,1,0:T(2,128)}) custom-call(s32[4,4,2]{2,1,0:T(4,128)S(1)} %copy.9.occ_ref, f32[6,6,4,8,128]{4,3,2,1,0:T(8,128)S(1)} %copy-done.1, f32[6,6,4,2,128]{4,3,2,1,0:T(2,128)S(1)} %copy-done.3, f32[4,4,2,128]{3,2,1,0:T(2,128)S(1)} %copy-done.6, f32[3,4,4,2,128]{4,3,2,1,0:T(2,128)S(1)} %copy-done.5, ...), custom_call_target="tpu_custom_call" | custom-call | tf_op jit(solution)/shard_map/pallas_call | solution.py:302
  (2 shorter events, 0.0 us)
Async XLA Ops:
  1.5 0.8 copy-start.11
  2.3 0.8 copy-start.5
  4.6 16.6 %copy-start.6 = (f32[4,4,2,128]{3,2,1,0:T(2,128)S(1)}, f32[4,4,2,128]{3,2,1,0:T(2,128)}, u32[]{:S(2)}) copy-start(f32[4,4,2,128]{3,2,1,0:T(2,128)} %mob_ref.3) | copy-start | bytes 49156
  21.2 1.1 copy-start
  22.3 0.9 copy-start.2
  23.2 51.5 %copy-start.1 = (f32[6,6,4,8,128]{4,3,2,1,0:T(8,128)S(1)}, f32[6,6,4,8,128]{4,3,2,1,0:T(8,128)}, u32[]{:S(2)}) copy-start(f32[6,6,4,8,128]{4,3,2,1,0:T(8,128)} %get-tuple-element.8.fix_ref) | copy-start | bytes 1769476
  23.2 51.5 %copy-start.3 = (f32[6,6,4,2,128]{4,3,2,1,0:T(2,128)S(1)}, f32[6,6,4,2,128]{4,3,2,1,0:T(2,128)}, u32[]{:S(2)}) copy-start(f32[6,6,4,2,128]{4,3,2,1,0:T(2,128)} %get-tuple-element.9.rest_ref) | copy-start | bytes 442372
  61.4 0.6 copy-start.7
  62.0 0.5 copy-start.9
  74.7 0.7 copy-start.10
  75.3 1.0 copy-start.4
  76.3 0.7 copy-start.8

commit v3 on v2

--- a/solution.py
+++ b/solution.py
@@ -94,7 +94,7 @@
             pltpu.SemaphoreType.DMA((messages,)),
             pltpu.SemaphoreType.DMA((2,)),
         ],
-        compiler_params=pltpu.CompilerParams(collective_id=collective, has_side_effects=True),
+        compiler_params=pltpu.CompilerParams(collective_id=collective, has_side_effects=True, vmem_limit_bytes=8 << 20),
     )(*args)
 
 
@@ -150,15 +150,15 @@
     row = lax.broadcasted_iota(jnp.int32, (8, slots), 0)
 
     def prepare(c, carry):
-        z = lax.rem(c, ext[2])
-        y = lax.rem(c // ext[2], ext[1])
-        x = c // (ext[2] * ext[1])
-        place = jnp.where(row < 3, spot(x, y, z) + offsets(row, (x, y, z), local), 0.0)
-        place_ref[x, y, z] = place
-        base_ref[x, y, z] = source_rows(fix_ref[x, y, z], place, row).astype(jnp.bfloat16)
+        x, y = c // ext[1], lax.rem(c, ext[1])
+        for z in range(ext[2]):
+            corner = offsets(row, (x, y, jnp.int32(z)), local)
+            place = jnp.where(row < 3, spot(x, y, z) + corner, 0.0)
+            place_ref[x, y, z] = place
+            base_ref[x, y, z] = source_rows(fix_ref[x, y, z], place, row).astype(jnp.bfloat16)
         return carry
 
-    lax.fori_loop(0, ext[0] * ext[1] * ext[2], prepare, 0)
+    lax.fori_loop(0, ext[0] * ext[1], prepare, 0)
 
     def one_cell(c, carry):
         z = lax.rem(c, local[2])
@@ -171,13 +171,13 @@
         lhs_ref[0] = jnp.where(lane < K_ROWS, turned, 0.0).astype(jnp.bfloat16)
         lhs_ref[1] = jnp.where(lane < K_ROWS, 0.0, turned).astype(jnp.bfloat16)
         acc_ref[...] = jnp.zeros_like(acc_ref)
-        groups = (occ_ref[x, y, z] + 31) // 32
-
-        for group in range(1, slots // 32 + 1):
+        groups = (occ_ref[x, y, z] + 15) // 16
+
+        for group in range(1, slots // 16 + 1):
 
             @pl.when(groups == group)
             def _():
-                rows = 32 * group
+                rows = 16 * group
                 lhs = jnp.concatenate([lhs_ref[0, :rows], lhs_ref[1, :rows]], axis=0)
 
                 for i, j in itertools.product(range(3), repeat=2):
@@ -265,7 +265,7 @@
         pltpu.VMEM((2, slots, 128), jnp.bfloat16),
         pltpu.VMEM((4, slots, slots), jnp.float32),
     ]
-    params = pltpu.CompilerParams(vmem_limit_bytes=48 << 20)
+    params = pltpu.CompilerParams(vmem_limit_bytes=16 << 20)
     rows = lambda lead, n: jax.ShapeDtypeStruct(lead + (n, slots), jnp.float32)
     field = jax.ShapeDtypeStruct((3,) + mobility.shape, jnp.float32)
     others = len(peers(shape))

time: 116 us -> 96.1 us (0.83)
  Pallas kernels: 106 us -> 92.6 us
  local copies, waits for them, and re-layouts: 8.64 us -> 2.59 us
    unnamed x25 -> x7, local copies, waits for them, and re-layouts: 7.03 us -> 1.62 us
    pallas_call x1, Pallas kernels: 39.2 us -> 34.1 us  [on_device(): pl.pallas_call(functools.partial(end_kernel, local, slots), out_shape=(fi...]
    pallas_call x1, Pallas kernels: 38.2 us -> 33.2 us  [on_device(): pl.pallas_call(functools.partial(start_kernel, local, slots), out_shape=(...]
    pallas_call x2, Pallas kernels: 28.7 us -> 25.2 us  [halo_call(): pl.pallas_call(kernel, out_shape=out_shape, in_specs=[vmem] * len(args),...]
where the time goes in v3:
time: 96.1 us; the launch traced here: 96 us
  Pallas kernels  92.6 us (96%)
  local copies, waits for them, and re-layouts  2.59 us (3%)
    pallas_call x1, Pallas kernels, on_device(): pl.pallas_call(functools.partial(end_kernel, local, slots), out_shape=(fi...  34.1 us
    pallas_call x1, Pallas kernels, on_device(): pl.pallas_call(functools.partial(start_kernel, local, slots), out_shape=(...  33.2 us
    pallas_call x2, Pallas kernels, halo_call(): pl.pallas_call(kernel, out_shape=out_shape, in_specs=[vmem] * len(args),...  25.2 us

profile of v3, /device:TPU:0, one launch (start us, length us, event | category | flops | bytes accessed | tf_op | source)
XLA Modules:
  0.0 96.0 jit_solution(11271233608321816269)
XLA Ops:
  0.6 0.8 copy.9.occ_ref
  1.4 0.1 compare_convert_fusion
  1.5 0.0 copy-start.2
  1.5 0.8 fusion.2
  2.3 0.0 copy-done.2
  2.3 0.0 copy-start
  2.3 0.8 copy-done
  3.2 0.2 stack.7.fix_ref
  3.4 0.0 copy-start.1
  3.4 14.8 %shard_map.68 = (f32[6,6,4,8,128]{4,3,2,1,0:T(8,128)S(1)}, f32[6,6,4,2,128]{4,3,2,1,0:T(2,128)S(1)}) custom-call(f32[4,4,2,8,128]{4,3,2,1,0:T(8,128)S(1)} %stack.7.fix_ref, f32[4,4,2,2,128]{4,3,2,1,0:T(2,128)S(1)} %pad_maximum_fusion.rest_ref), custom_call_target="tpu_custom_call" | custom-call | tf_op jit(solution)/shard_map/pallas_call | solution.py:87
  18.2 0.0 copy-done.1
  18.2 33.2 %shard_map.69 = (f32[4,4,2,4,128]{4,3,2,1,0:T(4,128)S(1)}, f32[1,128]{1,0:T(1,128)S(1)}) custom-call(s32[4,4,2]{2,1,0:T(4,128)S(1)} %copy.9.occ_ref, f32[6,6,4,8,128]{4,3,2,1,0:T(8,128)S(1)} %get-tuple-element.8.fix_ref, f32[6,6,4,2,128]{4,3,2,1,0:T(2,128)S(1)} %get-tuple-element.9.rest_ref, f32[4,4,2,128]{3,2,1,0:T(2,128)S(1)} %copy-done.1), custom_call_target="tpu_custom_call" | custom-call | tf_op jit(solution)/shard_map/pallas_call | solution.py:285
  51.5 10.4 %shard_map.70 = (f32[6,6,4,4,128]{4,3,2,1,0:T(4,128)S(1)}, f32[31,1,128]{2,1,0:T(1,128)S(1)}) custom-call(f32[4,4,2,4,128]{4,3,2,1,0:T(4,128)S(1)} %get-tuple-element.10.speed_ref, f32[1,128]{1,0:T(1,128)S(1)} %get-tuple-element.11.peak_ref), custom_call_target="tpu_custom_call" | custom-call | tf_op jit(solution)/shard_map/pallas_call | solution.py:87
  61.8 34.1 %shard_map.71 = (f32[3,4,4,2,128]{4,3,2,1,0:T(2,128)}, f32[3,4,4,2,128]{4,3,2,1,0:T(2,128)}) custom-call(s32[4,4,2]{2,1,0:T(4,128)S(1)} %copy.9.occ_ref, f32[6,6,4,8,128]{4,3,2,1,0:T(8,128)S(1)} %get-tuple-element.8.fix_ref, f32[6,6,4,2,128]{4,3,2,1,0:T(2,128)S(1)} %get-tuple-element.9.rest_ref, f32[4,4,2,128]{3,2,1,0:T(2,128)S(1)} %copy-done.1, ...), custom_call_target="tpu_custom_call" | custom-call | tf_op jit(solution)/shard_map/pallas_call | solution.py:302
  (3 shorter events, 0.0 us)
Async XLA Ops:
  1.5 0.8 copy-start.2
  2.3 0.8 copy-start
  3.4 14.8 %copy-start.1 = (f32[4,4,2,128]{3,2,1,0:T(2,128)S(1)}, f32[4,4,2,128]{3,2,1,0:T(2,128)}, u32[]{:S(2)}) copy-start(f32[4,4,2,128]{3,2,1,0:T(2,128)} %mob_ref.3) | copy-start | bytes 49156
